TPU v7x, 32 devices: a whole 2x2x4 slice. The times are simulated.
32 devices in a mesh: section: 2 (over core), ctx: 8 (over z, x), dp: 2 (over y).
Axes of the slice: x: 2, y: 2, z: 4, core: 2. Of those that a mesh axis runs over, the one named last changes fastest.
Arguments:
- hidden: bfloat16 [4, 2048, 5376], P(('section', 'dp'), 'ctx'), may hold values from -6 to 6
- frozen_query_rows: bfloat16 [4, 2048, 2048], P(('section', 'dp'), 'ctx'), may hold values from -12 to 12
- frozen_key_rows: bfloat16 [4, 2048, 1024], P(('section', 'dp'), 'ctx'), may hold values from -12 to 12
- frozen_value_rows: bfloat16 [4, 2048, 1024], P(('section', 'dp'), 'ctx'), may hold values from -6 to 6
- next_output_gradient: bfloat16 [4, 2048, 2048], P(('section', 'dp'), 'ctx'), may hold values from -0.011962891 to 0.011962891
- document_lengths: int32 [4, 16], P(('section', 'dp')), may hold values from 1 to 512, 2048 in all within a row
- document_adapter: int32 [4, 16], P(('section', 'dp')), may hold values from 0 to 3
- adapter_down_maps: bfloat16 [5376, 2, 4, 16], replicated, may hold values from -0.078125 to 0.078125
- adapter_up_maps: bfloat16 [2, 4, 16, 1024], replicated, may hold values from -1.5 to 1.5
Outputs:
- handed_on: bfloat16 [4, 2048, 2048], P(('section', 'dp'), 'ctx')
- down_map_gradient: float32 [5376, 2, 4, 16], replicated
- up_map_gradient: float32 [2, 4, 16, 1024], replicated
Inputs may be any that keep to these rules, and one draw needn't show every extreme that they name: `document_lengths`: each sequence's 16 lengths sum to 2048, and the longest is exactly 512.
All inputs are finite; a program needn't handle non-finite values.
Results may differ from a plain program's by a relative error of at most 0.016.
Values may be sent and summed in bfloat16 or wider, within the bound.
No kernel may reach another device: no remote copies, remote signals or barrier semaphores. Data moves between devices by JAX's collectives and lax.ppermute only.
A program may use at most 128 MiB of HBM per device.

v0:
```python
from functools import partial

import jax
import jax.numpy as jnp
import numpy as np
from jax import lax
from jax.experimental import pallas as pl
from jax.experimental.pallas import tpu as pltpu
from jax.sharding import PartitionSpec as P

HD = 128
WINDOW = 1024
SUB = 16
PIECES = (2, 2, 2, 2)

query_scale = 168.0 ** (-0.5)
adapter_scale = 0.5
log2e = 1.4426950408889634
rope_base = 10000.0
masked_score = -1e30
f32 = jnp.float32
bf16 = jnp.bfloat16


def permute_by(value, axis, steps):
    count = lax.axis_size(axis)
    first, last = max(0, -steps), min(count, count - steps)
    return lax.ppermute(value, axis, [(i, i + steps) for i in range(first, last)])


def permute_cyclic(value, axis, by):
    count = lax.axis_size(axis)
    return lax.ppermute(value, axis, [(i, (i + by) % count) for i in range(count)])


def permute_xor(value, axis, bit):
    count = lax.axis_size(axis)
    return lax.ppermute(value, axis, [(i, i ^ bit) for i in range(count)])


def window_blocks(own, steps, odd):
    chain = [own]
    for _ in range(steps):
        chain.append(permute_by(chain[-1], "ctx", 2))
    blocks = []
    for i in range(steps):
        payload = chosen(odd, chain[i], chain[i + 1])
        blocks.append(permute_xor(payload, "ctx", 1))
        blocks.append(chain[i + 1])
    return blocks


def choose_kernel(second_ref, a_ref, b_ref, out_ref):
    out_ref[...] = jnp.where(second_ref[0] == 0, a_ref[...], b_ref[...])


def chosen(second, a, b):
    resident = pl.BlockSpec(memory_space=pltpu.VMEM)
    return pl.pallas_call(
        choose_kernel,
        in_specs=[pl.BlockSpec(memory_space=pltpu.SMEM), resident, resident],
        out_specs=resident,
        out_shape=pltpu.VMEM(a.shape, a.dtype),
        compiler_params=pltpu.CompilerParams(vmem_limit_bytes=4 << 20),
        name="choose",
    )(second, in_vmem(a), in_vmem(b))


def tables_kernel(
    place_ref, lengths_ref, adapter_ref, freq_ref,
    mask_ref, own_mask_ref, bias_ref, cos_ref, sin_ref, *, adapters, rank,
):
    span, width = mask_ref.shape
    tok = bias_ref.shape[1]
    first = place_ref[1]

    def labels(position):
        docs = jnp.zeros(position.shape, jnp.int32)
        tenants = jnp.full(position.shape, adapter_ref[0, 0], jnp.int32)
        end = jnp.int32(0)
        for i in range(lengths_ref.shape[1]):
            end = end + lengths_ref[0, i]
            past = end <= position
            docs = docs + past.astype(jnp.int32)
            if i + 1 < lengths_ref.shape[1]:
                tenants = jnp.where(past, adapter_ref[0, i + 1], tenants)
        return docs, tenants

    key_pos = first + lax.broadcasted_iota(jnp.int32, (span, HD), 0)
    key_docs, key_tenants = labels(key_pos)
    lane = lax.broadcasted_iota(jnp.int32, (span, HD), 1)
    mask_ref[...] = ((lane // rank) % adapters == key_tenants).astype(f32).astype(bf16)
    pos = first + (span - tok) + lax.broadcasted_iota(jnp.int32, (SUB, tok), 1)
    docs, tenants = labels(pos)
    row = lax.broadcasted_iota(jnp.int32, (width, tok), 0)
    own_mask_ref[...] = ((row // rank) % adapters == tenants[:1]).astype(f32)
    for c in range(0, tok, HD):
        lanes = slice(c, c + HD)
        gap = pos[:1, lanes] - key_pos
        allowed = (key_docs == docs[:1, lanes]) & (gap >= 0) & (gap < WINDOW) & (key_pos >= 0)
        bias_ref[:, lanes] = jnp.where(allowed, 0.0, masked_score)
    angle = key_pos.astype(f32) * freq_ref[...]
    cos_ref[...] = jnp.cos(angle)
    sin = jnp.sin(angle)
    sin_ref[...] = jnp.where(lane < HD // 2, -sin, sin)


def tables(place, lengths, adapter, span, tok, adapters, rank):
    width = 2 * adapters * rank
    half = np.arange(HD // 2, dtype=np.float64) * 2.0 / HD
    freq = np.tile((rope_base ** -half).astype(np.float32), 2)[None]
    smem = pl.BlockSpec(memory_space=pltpu.SMEM)
    resident = pl.BlockSpec(memory_space=pltpu.VMEM)
    return pl.pallas_call(
        partial(tables_kernel, adapters=adapters, rank=rank),
        in_specs=[smem, smem, smem, resident],
        out_specs=[resident] * 5,
        out_shape=[
            pltpu.VMEM((span, width), bf16),
            pltpu.VMEM((width, tok), f32),
            pltpu.VMEM((span, tok), f32),
            pltpu.VMEM((span, HD), f32),
            pltpu.VMEM((span, HD), f32),
        ],
        compiler_params=pltpu.CompilerParams(vmem_limit_bytes=8 << 20),
        name="tables",
    )(place, lengths, adapter, jnp.asarray(freq))


def in_hbm(value):
    return pltpu.with_memory_space_constraint(value, pltpu.HBM)


def chunks_of(cols, parts):
    chunk = -(-cols // parts)
    chunk += chunk % 2
    return [slice(c * HD, min(c + chunk, cols) * HD) for c in range(0, cols, chunk)]


def pack_kernel(place_ref, hidden_hbm, down_hbm, key_hbm, val_hbm, *refs, pieces, lanes):
    messages = refs[: len(pieces)]
    place_out, hidden_ref, down_ref, sems = refs[len(pieces) :]
    place_out[0] = place_ref[0]
    place_out[1] = place_ref[1]
    loads, packs = [], []
    for k, cut in enumerate(lanes):
        loads.append(
            [
                pltpu.make_async_copy(hidden_hbm.at[:, cut], hidden_ref.at[:, cut], sems.at[2 * k]),
                pltpu.make_async_copy(down_hbm.at[:, cut], down_ref.at[:, cut], sems.at[2 * k + 1]),
            ]
        )
    at = 2 * len(lanes)
    begin = 0
    for heads, message in zip(pieces, messages):
        cut = slice(begin * HD, (begin + heads) * HD)
        begin += heads
        for j, rows in enumerate((key_hbm, val_hbm)):
            target = message.at[:, j * heads * HD : (j + 1) * heads * HD]
            packs.append(pltpu.make_async_copy(rows.at[:, cut], target, sems.at[at]))
            at += 1
    for pair in loads:
        for load in pair:
            load.start()
    for pack in packs:
        pack.start()
    low = None
    for pair, cut in zip(loads, lanes):
        for load in pair:
            load.wait()
        part = lax.dot_general(
            hidden_ref[:, cut],
            down_ref[:, cut],
            (((1,), (1,)), ((), ())),
            preferred_element_type=f32,
        )
        low = part if low is None else low + part
    messages[0][:, 2 * pieces[0] * HD :] = low.astype(bf16)
    for pack in packs:
        pack.wait()


def pack(place, hidden, down, keys, vals, pieces):
    tok, model_width = hidden.shape
    width = down.shape[0]
    lanes = chunks_of(model_width // HD, 6)
    *messages, place = pl.pallas_call(
        partial(pack_kernel, pieces=pieces, lanes=lanes),
        in_specs=[pl.BlockSpec(memory_space=pltpu.SMEM)] + [pl.BlockSpec(memory_space=pltpu.HBM)] * 4,
        out_specs=[pl.BlockSpec(memory_space=pltpu.VMEM)] * len(pieces)
        + [pl.BlockSpec(memory_space=pltpu.SMEM)],
        out_shape=[
            pltpu.VMEM((tok, 2 * heads * HD + (width if i == 0 else 0)), bf16)
            for i, heads in enumerate(pieces)
        ]
        + [pltpu.SMEM((2,), jnp.int32)],
        scratch_shapes=[
            pltpu.VMEM((tok, model_width), bf16),
            pltpu.VMEM((width, model_width), bf16),
            pltpu.SemaphoreType.DMA((2 * len(lanes) + 2 * len(pieces),)),
        ],
        compiler_params=pltpu.CompilerParams(vmem_limit_bytes=16 << 20),
        name="pack",
    )(place, in_hbm(hidden), in_hbm(down), in_hbm(keys), in_hbm(vals))
    return messages, place


def in_vmem(value):
    return pltpu.with_memory_space_constraint(value, pltpu.VMEM)


def attention_kernel(*refs, n_blocks, first_head, heads, tok, group, sub, rank, chained, is_last):
    m_refs = refs[:n_blocks]
    q_ref, up_ref, bias_ref, cos_ref, sin_ref, mask_ref, g_hbm = refs[n_blocks : n_blocks + 7]
    at = n_blocks + 7
    if chained:
        spread_ref, lg_in_ref = refs[at : at + 2]
        at += 4
    out_ref, u_ref = refs[at : at + 2]
    at += 2
    if not is_last:
        lg_ref = refs[at]
        at += 1
    else:
        low_refs = refs[at : at + n_blocks]
        at += n_blocks
    if not chained:
        spread_ref = refs[at]
        at += 1
    if is_last:
        lg_ref = refs[at]
        at += 1
    g_ref, g_sem = refs[at:]
    g_lanes = slice(first_head * group * HD, (first_head + heads) * group * HD)
    g_load = pltpu.make_async_copy(g_hbm.at[:, g_lanes], g_ref, g_sem)
    g_load.start()
    if not chained:
        low_lanes = slice(2 * heads * HD, None)
        low = jnp.concatenate([r[:, low_lanes] for r in m_refs], axis=0).astype(f32)
        spread_ref[...] = (low * mask_ref[...].astype(f32)).astype(bf16)
    spread = spread_ref[...]
    span = spread.shape[0]
    half = spread.shape[1] // 2
    cos, sin = cos_ref[...], sin_ref[...]
    dot = partial(lax.dot_general, preferred_element_type=f32)
    last, first = (((1,), (1,)), ((), ())), (((0,), (0,)), ((), ()))
    length = span - tok + sub
    subs = tok // sub

    def lanes_of(query_head):
        at = first_head * group + query_head
        return slice(at * HD, (at + 1) * HD)

    def up_of(h):
        lanes = slice((first_head + h) * HD, (first_head + h + 1) * HD)
        zero = jnp.zeros((up_ref.shape[1], HD), bf16)
        keys = jnp.concatenate([up_ref[0, :, lanes], zero], axis=1)
        vals = jnp.concatenate([zero, up_ref[1, :, lanes]], axis=1)
        return jnp.concatenate([keys, vals], axis=0)

    def prepare(h):
        shift = adapter_scale * jnp.dot(spread, up_of(h), preferred_element_type=f32)
        kc, vc = slice(h * HD, (h + 1) * HD), slice((heads + h) * HD, (heads + h + 1) * HD)
        key = jnp.concatenate([r[:, kc] for r in m_refs], axis=0).astype(f32) + shift[:, :HD]
        key = (key * cos + pltpu.roll(key, HD // 2, 1) * sin).astype(bf16)
        val = jnp.concatenate([r[:, vc] for r in m_refs], axis=0).astype(f32) + shift[:, HD:]
        return key, val.astype(bf16)

    def scored(h, i, key):
        cut = slice(i * sub, (i + 1) * sub)
        rows = slice(i * sub, i * sub + length)
        cq, sq = cos[span - tok + i * sub : span - tok + (i + 1) * sub], sin[span - tok + i * sub : span - tok + (i + 1) * sub]
        queries = []
        for j in range(group):
            q = q_ref[cut, lanes_of(h * group + j)].astype(f32)
            q = q * cq + pltpu.roll(q, HD // 2, 1) * sq
            queries.append((q * (query_scale * log2e)).astype(bf16))
        q = jnp.concatenate(queries, axis=0)
        bias = jnp.concatenate([bias_ref[rows, cut]] * group, axis=1)
        return q, dot(key[rows], q, last) + bias

    def forward(h, i, scores, val):
        cut = slice(i * sub, (i + 1) * sub)
        rows = slice(i * sub, i * sub + length)
        top = jnp.max(scores, axis=0, keepdims=True)
        probs = jnp.exp2(scores - top)
        scale = 1.0 / jnp.sum(probs, axis=0, keepdims=True)
        low_probs = probs.astype(bf16)
        out_t = (dot(val[rows], low_probs, first) * scale).astype(bf16)
        out = out_t.T
        gs = []
        for j in range(group):
            lanes = lanes_of(h * group + j)
            out_ref[cut, lanes] = out[j * sub : (j + 1) * sub]
            gs.append(g_ref[cut, (h * group + j) * HD : (h * group + j + 1) * HD])
        g_t = (jnp.concatenate(gs, axis=0).T.astype(f32) * scale).astype(bf16)
        drift = jnp.sum(out_t.astype(f32) * g_t.astype(f32), axis=0, keepdims=True)
        dprob = jnp.dot(val[rows], g_t, preferred_element_type=f32)
        return probs, low_probs, g_t, drift, dprob

    def backward(q, state):
        probs, low_probs, g_t, drift, dprob = state
        dscore = (probs * (dprob - drift)).astype(bf16)
        return jnp.dot(dscore, q, preferred_element_type=f32), dot(low_probs, g_t, last)

    def overlapped(parts):
        rows = []
        for j in range(span // sub):
            here = [p[(j - i) * sub : (j - i + 1) * sub] for i, p in enumerate(parts) if 0 <= j - i < length // sub]
            rows.append(sum(here[1:], here[0]))
        return jnp.concatenate(rows, axis=0)

    def finish(h, parts):
        dkey = (1.0 / log2e) * overlapped([p[0] for p in parts])
        dval = overlapped([p[1] for p in parts])
        dkey = dkey * cos - pltpu.roll(dkey, HD // 2, 1) * sin
        both = jnp.concatenate([dkey.astype(bf16), dval.astype(bf16)], axis=1)
        lg = dot(both, up_of(h), last)
        if h > 0:
            lg_ref[...] += lg
        else:
            lg_ref[...] = lg_in_ref[...] + lg if chained else lg
        u = adapter_scale * dot(spread, both, first)
        head_lanes = slice((first_head + h) * HD, (first_head + h + 1) * HD)
        u_ref[0, :, head_lanes] = u[:half, :HD].astype(bf16)
        u_ref[1, :, head_lanes] = u[half:, HD:].astype(bf16)

    units = [(h, i) for h in range(heads) for i in range(subs)]
    prepared, scores, states, grads = {}, {}, {}, {}
    for t in range(len(units) + 2):
        if t < len(units):
            h, i = units[t]
            if i == 0:
                prepared[h] = prepare(h)
            scores[h, i] = scored(h, i, prepared[h][0])
        if t == 1:
            g_load.wait()
        if 0 <= t - 1 < len(units):
            h, i = units[t - 1]
            states[h, i] = forward(h, i, scores[h, i][1], prepared[h][1])
        if 0 <= t - 2 < len(units):
            h, i = units[t - 2]
            grads.setdefault(h, []).append(backward(scores[h, i][0], states[h, i]))
            if i == subs - 1:
                finish(h, grads[h])
    if is_last:
        masked = (adapter_scale * lg_ref[...] * mask_ref[...].astype(f32)).astype(bf16)
        compact = dot(picks(2 * half, rank), masked, last)
        for j, ref in enumerate(low_refs):
            ref[...] = compact[:, j * tok : (j + 1) * tok].astype(bf16)


def picks(width, rank):
    row = lax.broadcasted_iota(jnp.int32, (2 * rank, width), 0)
    col = lax.broadcasted_iota(jnp.int32, (2 * rank, width), 1)
    hit = (row // rank == col // (width // 2)) & (row % rank == col % rank)
    return hit.astype(f32).astype(bf16)


def attention(blocks, first_head, heads, carried, is_last, mask, q_rows, g_rows, ups, bias, cos, sin, rank):
    tok = q_rows.shape[0]
    _, half, kv_width = ups.shape
    kv_heads, width = kv_width // HD, 2 * half
    group = q_rows.shape[1] // (kv_heads * HD)
    n_blocks = len(blocks)
    span = bias.shape[0]
    sub = HD if tok % HD == 0 else tok
    operands = [in_vmem(x) for x in (*blocks, q_rows, ups, bias, cos, sin, mask)]
    operands.append(in_hbm(g_rows))
    aliases = {}
    resident = [pl.BlockSpec(memory_space=pltpu.VMEM)]
    in_specs = resident * (len(operands) - 1) + [pl.BlockSpec(memory_space=pltpu.HBM)]
    if carried is not None:
        at = len(operands)
        aliases = {at + 2: 0, at + 3: 1}
        if not is_last:
            aliases[at + 1] = 2
        out, u, lg, spread = carried
        operands += [in_vmem(x) for x in (spread, lg, out, u)]
        in_specs = in_specs + resident * 4
    out_shape = [pltpu.VMEM(q_rows.shape, bf16), pltpu.VMEM((2, half, kv_heads * HD), bf16)]
    scratch = []
    if is_last:
        out_shape += [pltpu.VMEM((2 * rank, tok), bf16)] * n_blocks
        scratch = [pltpu.VMEM((span, width), f32)]
    else:
        out_shape.append(pltpu.VMEM((span, width), f32))
    if carried is None:
        out_shape.append(pltpu.VMEM((span, width), bf16))
    work = heads * group * tok * (span - tok + sub) * HD * 2 * 6
    result = pl.pallas_call(
        partial(
            attention_kernel,
            n_blocks=n_blocks,
            first_head=first_head,
            heads=heads,
            tok=tok,
            group=group,
            sub=sub,
            rank=rank,
            chained=carried is not None,
            is_last=is_last,
        ),
        in_specs=in_specs,
        out_specs=resident * len(out_shape),
        out_shape=out_shape,
        scratch_shapes=scratch
        + [pltpu.VMEM((tok, heads * group * HD), bf16), pltpu.SemaphoreType.DMA(())],
        input_output_aliases=aliases,
        compiler_params=pltpu.CompilerParams(vmem_limit_bytes=28 << 20),
        cost_estimate=pl.CostEstimate(flops=work, transcendentals=0, bytes_accessed=heads * tok * HD * 20),
        name="attention",
    )(*operands)
    if is_last:
        return result
    return (*result[:3], result[3] if carried is None else spread)


def product_kernel(*refs, n_recv, lanes, up_cols):
    side_ref, own_ref = refs[:2]
    recv = refs[2 : 2 + n_recv]
    mask_ref, up_ref, handed_ref, hidden_hbm = refs[2 + n_recv : 6 + n_recv]
    keep_ref, send_ref, handed_out, hidden_ref, sems = refs[6 + n_recv :]
    loads = [
        pltpu.make_async_copy(hidden_hbm.at[:, cut], hidden_ref.at[:, cut], sems.at[k])
        for k, cut in enumerate(lanes)
    ]
    handing = pltpu.make_async_copy(handed_ref, handed_out, sems.at[len(loads)])
    for load in loads:
        load.start()
    handing.start()
    side = side_ref[0]
    total = own_ref[...].astype(f32)
    for r in recv:
        total = total + r[...].astype(f32)
    width = mask_ref.shape[0]
    half = width // 2
    cols = hidden_ref.shape[1] // HD
    total = lax.dot_general(
        picks(width, total.shape[0] // 2),
        total.astype(bf16),
        (((0,), (0,)), ((), ())),
        preferred_element_type=f32,
    )
    total = total * mask_ref[...]
    swapped = jnp.concatenate([total[half:], total[:half]], axis=0)
    total = jnp.where(side == 0, total, swapped).astype(bf16)
    per_row = cols + up_cols
    rows = half // SUB
    for h in range(up_cols):
        for r in range(rows):
            where = (slice(r * SUB, (r + 1) * SUB), slice(h * HD, (h + 1) * HD))
            keep_ref[r * per_row + cols + h] = up_ref[(side,) + where]
            send_ref[r * per_row + cols + h] = up_ref[(1 - side,) + where]
    used = rows * per_row
    if keep_ref.shape[0] > used:
        rest = keep_ref.shape[0] - used
        keep_ref[pl.ds(used, rest)] = jnp.zeros((rest, SUB, HD), bf16)
        send_ref[pl.ds(used, rest)] = jnp.zeros((rest, SUB, HD), bf16)
    step = 2 if cols % 2 == 0 else 1
    starts = [cut.start // HD for cut in lanes]
    for c in range(0, cols, step):
        if c in starts:
            loads[starts.index(c)].wait()
        w = jnp.dot(
            total, hidden_ref[:, c * HD : (c + step) * HD], preferred_element_type=f32
        ).astype(bf16)
        for j in range(step):
            for r in range(rows):
                tile = w[:, j * HD : (j + 1) * HD]
                keep_ref[r * per_row + c + j] = tile[r * SUB : (r + 1) * SUB]
                send_ref[r * per_row + c + j] = tile[half + r * SUB : half + (r + 1) * SUB]
    handing.wait()


def merge_kernel(keep_ref, recv_ref, *out_refs):
    at = 0
    for ref in out_refs:
        rows = slice(at, at + ref.shape[0])
        ref[...] = (keep_ref[rows].astype(f32) + recv_ref[rows].astype(f32)).astype(bf16)
        at += ref.shape[0]


def assemble_kernel(
    scalars_ref, ma_ref, mb_ref, ra_ref, rb_ref, w_hbm, u_hbm, w_ref, u_ref, sems, *, cols, rows
):
    side, me_a, me_b = scalars_ref[0], scalars_ref[1], scalars_ref[2]
    n_a, a = ma_ref.shape[:2]
    b = mb_ref.shape[1]
    up_cols = u_ref.shape[1] // HD
    per_row = cols + up_cols
    stores = []
    for r in range(rows):
        starts = [pl.multiple_of((m * rows + r) * SUB, SUB) for m in (side, 1 - side)]
        for c in range(per_row):
            t = r * per_row + c
            if t < n_a * a:
                mine, theirs, piece, off = ma_ref, ra_ref, (t // a) ^ me_a, t % a
            else:
                t -= n_a * a
                mine, theirs, piece, off = mb_ref, rb_ref, (t // b) ^ me_b, t % b
            for src, at in zip((mine, theirs), starts):
                tile = src[piece, off].astype(f32)
                if c < cols:
                    w_ref[pl.ds(at, SUB), c * HD : (c + 1) * HD] = tile
                else:
                    u_ref[pl.ds(at, SUB), (c - cols) * HD : (c - cols + 1) * HD] = tile
        for at in starts:
            band = pl.ds(at, SUB)
            stores.append(pltpu.make_async_copy(w_ref.at[band], w_hbm.at[band], sems.at[len(stores)]))
            stores[-1].start()
    stores.append(pltpu.make_async_copy(u_ref, u_hbm, sems.at[len(stores)]))
    stores[-1].start()
    for store in stores:
        store.wait()


def axis_bits(axis):
    bits, bit = [], 1
    while bit < lax.axis_size(axis):
        bits.append((axis, bit))
        bit *= 2
    return bits


def bit_of(stage):
    axis, bit = stage
    return ((lax.axis_index(axis) & bit) != 0).astype(jnp.int32)


def direct_peers(axis, bits):
    masks = [0]
    for bit in bits:
        masks = masks + [m | bit for m in masks]
    me = jnp.int32(0)
    for bit in reversed(bits):
        me = me * 2 + bit_of((axis, bit))
    return masks, me


def direct_scatter(tiles, axis, bits):
    masks, me = direct_peers(axis, bits)
    total = lax.dynamic_index_in_dim(tiles, me, 0, keepdims=False).astype(f32)
    for j in range(1, len(masks)):
        part = lax.dynamic_index_in_dim(tiles, me ^ j, 0, keepdims=False)
        total = total + permute_xor(part, axis, masks[j]).astype(f32)
    return total.astype(bf16)


def direct_gather(tiles, axis, bits):
    masks, _ = direct_peers(axis, bits)
    return jnp.stack([tiles] + [permute_xor(tiles, axis, m) for m in masks[1:]])


def scatter_stage(tiles, stage):
    n = tiles.shape[0] // 2
    bit = bit_of(stage)
    send = lax.dynamic_slice_in_dim(tiles, (1 - bit) * n, n, 0)
    keep = lax.dynamic_slice_in_dim(tiles, bit * n, n, 0)
    recv = permute_xor(send, *stage)
    return (keep.astype(f32) + recv.astype(f32)).astype(bf16)


def gather_stage(tiles, stage):
    return jnp.concatenate([tiles, permute_xor(tiles, *stage)], axis=0)


def step(
    hidden,
    frozen_query_rows,
    frozen_key_rows,
    frozen_value_rows,
    next_output_gradient,
    document_lengths,
    document_adapter,
    adapter_down_maps,
    adapter_up_maps,
):
    tok, model_width = hidden.shape[1:]
    kv_width = frozen_key_rows.shape[2]
    kv_heads = kv_width // HD
    _, adapters, rank, _ = adapter_up_maps.shape
    width = 2 * adapters * rank
    half = width // 2
    ctx_index, ctx_size = lax.axis_index("ctx"), lax.axis_size("ctx")
    longest = tok * ctx_size // 4
    reach = min(-(-(min(WINDOW, longest) - 1) // tok), ctx_size - 1)
    steps = (reach + 1) // 2

    pieces = PIECES if sum(PIECES) == kv_heads else (kv_heads,)
    down = adapter_down_maps.reshape(model_width, width).T
    place = jnp.stack([ctx_index % 2, (ctx_index - 2 * steps) * tok]).astype(jnp.int32)
    messages, place = pack(place, hidden[0], down, frozen_key_rows[0], frozen_value_rows[0], pieces)
    parts = [window_blocks(m, steps, place)[::-1] + [m] for m in messages]
    returned = permute_cyclic(next_output_gradient, "section", -1)

    span = (2 * steps + 1) * tok
    mask, own_mask, bias, cos, sin = tables(
        place, document_lengths, document_adapter, span, tok, adapters, rank
    )
    up_rows = adapter_up_maps.reshape(2, half, kv_width)
    carried = None
    for i, heads in enumerate(pieces):
        carried = attention(
            parts[i],
            sum(pieces[:i]),
            heads,
            carried,
            i == len(pieces) - 1,
            mask,
            frozen_query_rows[0],
            returned[0],
            up_rows,
            bias,
            cos,
            sin,
            rank,
        )
    out, ups = carried[:2]
    lows = carried[2:]
    received = [permute_by(low, "ctx", j - 2 * steps) for j, low in enumerate(lows[:-1])]
    handed = permute_cyclic(out, "section", 1)[None]

    other = (
        axis_bits("ctx")[:1] + axis_bits("dp"),
        axis_bits("dp") + axis_bits("ctx")[:1],
    )
    tail = [bit for _, bit in axis_bits("ctx")[1:]]
    group = lax.axis_size("ctx") * lax.axis_size("dp")
    cols, up_cols, rows = model_width // HD, kv_heads, half // SUB
    units = -(-(rows * (cols + up_cols)) // group)
    a = (units + 1) // 2
    b = units - a
    side = lax.axis_index("section").astype(jnp.int32)
    smem = pl.BlockSpec(memory_space=pltpu.SMEM)
    vmem = pl.BlockSpec(memory_space=pltpu.VMEM)
    any_space = pl.BlockSpec(memory_space=pl.ANY)
    lanes = chunks_of(cols, 3)
    tile_shape = (units * group, SUB, HD)
    keep, send, handed = pl.pallas_call(
        partial(product_kernel, n_recv=len(received), lanes=lanes, up_cols=up_cols),
        in_specs=[smem] + [vmem] * (4 + len(received)) + [pl.BlockSpec(memory_space=pltpu.HBM)],
        out_specs=[vmem, vmem, any_space],
        out_shape=[
            pltpu.VMEM(tile_shape, bf16),
            pltpu.VMEM(tile_shape, bf16),
            jax.ShapeDtypeStruct(handed.shape, bf16),
        ],
        scratch_shapes=[
            pltpu.VMEM((tok, model_width), bf16),
            pltpu.SemaphoreType.DMA((len(lanes) + 1,)),
        ],
        compiler_params=pltpu.CompilerParams(vmem_limit_bytes=16 << 20),
        name="product",
    )(
        side[None],
        *[in_vmem(x) for x in (lows[-1], *received, own_mask, ups, handed)],
        in_hbm(hidden[0]),
    )
    recv = permute_cyclic(send, "section", 1)
    colours = pl.pallas_call(
        merge_kernel,
        in_specs=[vmem, vmem],
        out_specs=[vmem, vmem],
        out_shape=[pltpu.VMEM((n * group, SUB, HD), bf16) for n in (a, b)],
        compiler_params=pltpu.CompilerParams(vmem_limit_bytes=8 << 20),
        name="merge",
    )(in_vmem(keep), in_vmem(recv))
    for k in range(len(other[0])):
        colours = [scatter_stage(colours[c], other[c][k]) for c in range(2)]
    rounds = [tail[k : k + 2] for k in range(0, len(tail), 2)]
    members = group >> len(other[0])
    joined = jnp.concatenate([c.reshape(members, -1, SUB, HD) for c in colours], axis=1)
    for bits in rounds:
        joined = joined.reshape(2 ** len(bits), -1, a + b, SUB, HD)
        joined = direct_scatter(joined, "ctx", bits)
    joined = joined.reshape(a + b, SUB, HD)
    ids = []
    for c in range(2):
        me = jnp.int32(0)
        for stage in other[c]:
            me = me * 2 + bit_of(stage)
        for bits in rounds:
            me = me * 2 ** len(bits) + direct_peers("ctx", bits)[1]
        ids.append(me)
    joined = joined[None]
    for bits in reversed(rounds):
        joined = direct_gather(joined, "ctx", bits).reshape(-1, a + b, SUB, HD)
    colours = [
        joined[:, :a].reshape(-1, SUB, HD),
        joined[:, a:].reshape(-1, SUB, HD),
    ]
    for k in reversed(range(len(other[0]))):
        colours = [gather_stage(colours[c], other[c][k]) for c in range(2)]
    theirs = [permute_cyclic(t, "section", 1) for t in colours]
    shapes = [(group, a, SUB, HD), (group, b, SUB, HD)]
    w, u = pl.pallas_call(
        partial(assemble_kernel, cols=cols, rows=rows),
        in_specs=[smem] + [vmem] * 4,
        out_specs=[any_space, any_space],
        out_shape=[
            jax.ShapeDtypeStruct((width, model_width), f32),
            jax.ShapeDtypeStruct((width, kv_width), f32),
        ],
        scratch_shapes=[
            pltpu.VMEM((width, model_width), f32),
            pltpu.VMEM((width, kv_width), f32),
            pltpu.SemaphoreType.DMA((2 * rows + 1,)),
        ],
        compiler_params=pltpu.CompilerParams(vmem_limit_bytes=16 << 20),
        name="assemble",
    )(
        jnp.stack([side, ids[0], ids[1]]),
        in_vmem(colours[0].reshape(shapes[0])),
        in_vmem(colours[1].reshape(shapes[1])),
        in_vmem(theirs[0].reshape(shapes[0])),
        in_vmem(theirs[1].reshape(shapes[1])),
    )
    down_map_gradient = w.T.reshape(model_width, 2, adapters, rank)
    up_map_gradient = u.reshape(2, adapters, rank, kv_width)
    return (handed, down_map_gradient, up_map_gradient)


def solution(mesh):
    return jax.shard_map(
        step,
        mesh=mesh,
        in_specs=(
            P(("section", "dp"), "ctx", None),
            P(("section", "dp"), "ctx", None),
            P(("section", "dp"), "ctx", None),
            P(("section", "dp"), "ctx", None),
            P(("section", "dp"), "ctx", None),
            P(("section", "dp"), None),
            P(("section", "dp"), None),
            P(),
            P(),
        ),
        out_specs=(P(("section", "dp"), "ctx", None), P(), P()),
        check_vma=False,
    )
```

profile of v0, /device:TPU:0, one launch (start us, length us, event | category | flops | bytes accessed | tf_op | source)
XLA Modules:
  0.0 114.3 jit_solution(9176731443126339479)
XLA Ops:
  1.3 3.8 %pack.1 = (bf16[256,640]{1,0:T(8,128)(2,1)S(1)}, bf16[256,512]{1,0:T(8,128)(2,1)S(1)}, bf16[256,512]{1,0:T(8,128)(2,1)S(1)}, bf16[256,512]{1,0:T(8,128)(2,1)S(1)}, s32[2]{0:T(128)S(4)}) custom-call(s32[2]{0:T(128)S(1)} %pad_add_fusion.place_ref, bf16[256,5376]{1,0:T(8,128)(2,1)} %bitcast.50, bf16[128,5376]{1,0:T(8,128)(2,1)} %bitcast.52, ...), custom_call_target="tpu_custom_call" | custom-call | tf_op jit(solution)/shard_map/pack/pallas_call | solution.py:187
  5.1 4.6 %collective-permute-start.3 = (bf16[256,640]{1,0:T(8,128)(2,1)S(1)}, bf16[256,640]{1,0:T(8,128)(2,1)S(1)}, u32[]{:S(2)}, u32[]{:S(2)}) collective-permute-start(bf16[256,640]{1,0:T(8,128)(2,1)S(1)} %get-tuple-element.41.a_ref.refs_2_), channel_id=1, source_target_pairs={{0,4},{2,6},{4,8},{6,10},{8,12},{10,14},{1,5},{3,7},{5,9},{7,11},{... | collective-permute-start | bytes 983048 | tf_op jit(solution)/shard_map/ppermute | solution.py:28
  9.8 3.5 %collective-permute-start.7 = (bf16[256,512]{1,0:T(8,128)(2,1)S(1)}, bf16[256,512]{1,0:T(8,128)(2,1)S(1)}, u32[]{:S(2)}, u32[]{:S(2)}) collective-permute-start(bf16[256,512]{1,0:T(8,128)(2,1)S(1)} %get-tuple-element.44.a_ref.refs_2_), channel_id=1, source_target_pairs={{0,4},{2,6},{4,8},{6,10},{8,12},{10,14},{1,5},{3,7},{5,9},{7,11},{... | collective-permute-start | bytes 786440 | tf_op jit(solution)/shard_map/ppermute | solution.py:28
  13.2 3.5 %collective-permute-start.5 = (bf16[256,512]{1,0:T(8,128)(2,1)S(1)}, bf16[256,512]{1,0:T(8,128)(2,1)S(1)}, u32[]{:S(2)}, u32[]{:S(2)}) collective-permute-start(bf16[256,512]{1,0:T(8,128)(2,1)S(1)} %get-tuple-element.43.a_ref.refs_2_), channel_id=1, source_target_pairs={{0,4},{2,6},{4,8},{6,10},{8,12},{10,14},{1,5},{3,7},{5,9},{7,11},{... | collective-permute-start | bytes 786440 | tf_op jit(solution)/shard_map/ppermute | solution.py:28
  19.4 4.4 %collective-permute-start = (bf16[256,512]{1,0:T(8,128)(2,1)S(1)}, bf16[256,512]{1,0:T(8,128)(2,1)S(1)}, u32[]{:S(2)}, u32[]{:S(2)}) collective-permute-start(bf16[256,512]{1,0:T(8,128)(2,1)S(1)} %get-tuple-element.35.a_ref.refs_2_), channel_id=1, source_target_pairs={{0,4},{2,6},{4,8},{6,10},{8,12},{10,14},{1,5},{3,7},{5,9},{7,11},{... | collective-permute-start | bytes 786440 | tf_op jit(solution)/shard_map/ppermute | solution.py:28
  25.0 4.0 %collective-permute-done.5.b_ref.refs_0_ = bf16[256,512]{1,0:T(8,128)(2,1)S(1)} collective-permute-done((bf16[256,512]{1,0:T(8,128)(2,1)S(1)}, bf16[256,512]{1,0:T(8,128)(2,1)S(1)}, u32[]{:S(2)}, u32[]{:S(2)}) %collective-permute-start.5) | collective-permute-done | bytes 262176 | tf_op jit(solution)/shard_map/ppermute | solution.py:28
  30.6 3.2 %tables.1 = (bf16[768,128]{1,0:T(8,128)(2,1)S(1)}, f32[128,256]{1,0:T(8,128)S(1)}, f32[768,256]{1,0:T(8,128)S(1)}, f32[768,128]{1,0:T(8,128)S(1)}, f32[768,128]{1,0:T(8,128)S(1)}) custom-call(s32[2]{0:T(128)S(4)} %get-tuple-element.36.second_ref.place_ref, s32[1,16]{1,0:T(1,128)S(1)} %copy-done.2, s32[1,16]{1,0:T(1,128)S(1)} %copy-done.3, f32[1,128]{1,0:T(1,128)S(1)} %copy-done.4), custom_call_target="tpu_custom_call" | custom-call | tf_op jit(solution)/shard_map/tables/pallas_call | solution.py:114
  36.8 3.5 %attention.4 = (bf16[256,2048]{1,0:T(8,128)(2,1)S(1)}, bf16[2,64,1024]{2,1,0:T(8,128)(2,1)S(1)}, f32[768,128]{1,0:T(8,128)S(1)}, bf16[768,128]{1,0:T(8,128)(2,1)S(1)}) custom-call(bf16[256,640]{1,0:T(8,128)(2,1)S(1)} %collective-permute-done.3.b_ref.refs_0_, bf16[256,640]{1,0:T(8,128)(2,1)S(1)} %collective-permute-done.4.refs_1_, ...), custom_call_target="tpu_custom_call" | custom-call | flops 1006632960 | bytes 1310720 | tf_op jit(solution)/shard_map/attention/pallas_call | solution.py:391
  40.2 3.9 %attention.5 = (bf16[256,2048]{1,0:T(8,128)(2,1)S(1)}, bf16[2,64,1024]{2,1,0:T(8,128)(2,1)S(1)}, f32[768,128]{1,0:T(8,128)S(1)}) custom-call(bf16[256,512]{1,0:T(8,128)(2,1)S(1)} %collective-permute-done.7.b_ref.refs_0_, bf16[256,512]{1,0:T(8,128)(2,1)S(1)} %collective-permute-done.8.refs_1_, ...), custom_call_target="tpu_custom_call", output_to_operand_aliasing={{0}: (12, {}), {1}: (13, {}), {2}: (11, {})} | custom-call | flops 1006632960 | bytes 1310720 | tf_op jit(solution)/shard_map/attention/pallas_call | solution.py:391
  44.1 4.1 %attention.6 = (bf16[256,2048]{1,0:T(8,128)(2,1)S(1)}, bf16[2,64,1024]{2,1,0:T(8,128)(2,1)S(1)}, f32[768,128]{1,0:T(8,128)S(1)}) custom-call(bf16[256,512]{1,0:T(8,128)(2,1)S(1)} %collective-permute-done.5.b_ref.refs_0_, bf16[256,512]{1,0:T(8,128)(2,1)S(1)} %collective-permute-done.6.refs_1_, ...), custom_call_target="tpu_custom_call", output_to_operand_aliasing={{0}: (12, {}), {1}: (13, {}), {2}: (11, {})} | custom-call | flops 1006632960 | bytes 1310720 | tf_op jit(solution)/shard_map/attention/pallas_call | solution.py:391
  48.2 4.0 %attention.7 = (bf16[256,2048]{1,0:T(8,128)(2,1)S(1)}, bf16[2,64,1024]{2,1,0:T(8,128)(2,1)S(1)}, bf16[32,256]{1,0:T(8,128)(2,1)S(1)}, bf16[32,256]{1,0:T(8,128)(2,1)S(1)}, bf16[32,256]{1,0:T(8,128)(2,1)S(1)}) custom-call(bf16[256,512]{1,0:T(8,128)(2,1)S(1)} %collective-permute-done.b_ref.refs_0_, ...), custom_call_target="tpu_custom_call", output_to_operand_aliasing={{0}: (12, {}), {1}: (13, {})} | custom-call | flops 1006632960 | bytes 1310720 | tf_op jit(solution)/shard_map/attention/pallas_call | solution.py:391
  54.8 3.0 %collective-permute-done.10.refs_3_ = bf16[32,256]{1,0:T(8,128)(2,1)S(1)} collective-permute-done((bf16[32,256]{1,0:T(8,128)(2,1)S(1)}, bf16[32,256]{1,0:T(8,128)(2,1)S(1)}, u32[]{:S(2)}, u32[]{:S(2)}) %collective-permute-start.10) | collective-permute-done | bytes 16416 | tf_op jit(solution)/shard_map/ppermute | solution.py:28
  57.9 2.4 %collective-permute-done.9.refs_2_ = bf16[32,256]{1,0:T(8,128)(2,1)S(1)} collective-permute-done((bf16[32,256]{1,0:T(8,128)(2,1)S(1)}, bf16[32,256]{1,0:T(8,128)(2,1)S(1)}, u32[]{:S(2)}, u32[]{:S(2)}) %collective-permute-start.9) | collective-permute-done | bytes 16416 | tf_op jit(solution)/shard_map/ppermute | solution.py:28
  60.2 2.6 %product.1 = (bf16[208,16,128]{2,1,0:T(8,128)(2,1)S(1)}, bf16[208,16,128]{2,1,0:T(8,128)(2,1)S(1)}, bf16[1,256,2048]{2,1,0:T(8,128)(2,1)}) custom-call(s32[1]{0:T(128)} %bitcast.refs_0_, bf16[32,256]{1,0:T(8,128)(2,1)S(1)} %get-tuple-element.54.refs_1_, bf16[32,256]{1,0:T(8,128)(2,1)S(1)} %collective-permute-done.9.refs_2_, ...), custom_call_target="tpu_custom_call" | custom-call | tf_op jit(solution)/shard_map/product/pallas_call | solution.py:640
  62.9 2.4 %collective-permute-done.12.recv_ref = bf16[208,16,128]{2,1,0:T(8,128)(2,1)S(1)} collective-permute-done((bf16[208,16,128]{2,1,0:T(8,128)(2,1)S(1)}, bf16[208,16,128]{2,1,0:T(8,128)(2,1)S(1)}, u32[]{:S(2)}, u32[]{:S(2)}) %collective-permute-start.12) | collective-permute-done | bytes 852000 | tf_op jit(solution)/shard_map/ppermute | solution.py:33
  69.2 3.3 %collective-permute-done.15 = bf16[48,16,128]{2,1,0:T(8,128)(2,1)S(1)} collective-permute-done((bf16[48,16,128]{2,1,0:T(8,128)(2,1)S(1)}, bf16[48,16,128]{2,1,0:T(8,128)(2,1)S(1)}, u32[]{:S(2)}, u32[]{:S(2)}) %collective-permute-start.15) | collective-permute-done | bytes 196640 | tf_op jit(solution)/shard_map/ppermute | solution.py:38
  77.3 2.4 %collective-permute-done.14 = bf16[28,16,128]{2,1,0:T(8,128)(2,1)S(1)} collective-permute-done((bf16[28,16,128]{2,1,0:T(8,128)(2,1)S(1)}, bf16[28,16,128]{2,1,0:T(8,128)(2,1)S(1)}, u32[]{:S(2)}, u32[]{:S(2)}) %collective-permute-start.14) | collective-permute-done | bytes 114720 | tf_op jit(solution)/shard_map/ppermute | solution.py:38
  79.8 2.1 %collective-permute-start.17 = (bf16[1,13,16,128]{3,2,1,0:T(8,128)(2,1)S(1)}, bf16[1,13,16,128]{3,2,1,0:T(8,128)(2,1)S(1)}, u32[]{:S(2)}, u32[]{:S(2)}) collective-permute-start(bf16[1,13,16,128]{3,2,1,0:T(8,128)(2,1)S(1)} %get-tuple-element.67), channel_id=1, source_target_pairs={{0,4},{2,6},{4,0},{6,2},{8,12},{10,14},{12,8},{14,10},{1,5},{3,7},... | collective-permute-start | bytes 159752 | tf_op jit(solution)/shard_map/ppermute | solution.py:38
  84.5 3.0 %collective-permute-done.18 = bf16[1,13,16,128]{3,2,1,0:T(8,128)(2,1)S(1)} collective-permute-done((bf16[1,13,16,128]{3,2,1,0:T(8,128)(2,1)S(1)}, bf16[1,13,16,128]{3,2,1,0:T(8,128)(2,1)S(1)}, u32[]{:S(2)}, u32[]{:S(2)}) %collective-permute-start.18) | collective-permute-done | bytes 53280 | tf_op jit(solution)/shard_map/ppermute | solution.py:38
  91.3 2.4 %collective-permute-start.22 = (bf16[1,13,16,128]{3,2,1,0:T(8,128)(2,1)S(1)}, bf16[1,13,16,128]{3,2,1,0:T(8,128)(2,1)S(1)}, u32[]{:S(2)}, u32[]{:S(2)}) collective-permute-start(bf16[1,13,16,128]{3,2,1,0:T(8,128)(2,1)S(1)} %add_convert_fusion.4), channel_id=1, source_target_pairs={{0,12},{2,14},{4,8},{6,10},{8,4},{10,6},{12,0},{14,2},{1,13},{3,15... | collective-permute-start | bytes 159752 | tf_op jit(solution)/shard_map/ppermute | solution.py:38
  95.0 2.3 %collective-permute-done.22 = bf16[1,13,16,128]{3,2,1,0:T(8,128)(2,1)S(1)} collective-permute-done((bf16[1,13,16,128]{3,2,1,0:T(8,128)(2,1)S(1)}, bf16[1,13,16,128]{3,2,1,0:T(8,128)(2,1)S(1)}, u32[]{:S(2)}, u32[]{:S(2)}) %collective-permute-start.22) | collective-permute-done | bytes 53280 | tf_op jit(solution)/shard_map/ppermute | solution.py:38
  99.5 3.6 %collective-permute-done.23 = bf16[28,16,128]{2,1,0:T(8,128)(2,1)S(1)} collective-permute-done((bf16[28,16,128]{2,1,0:T(8,128)(2,1)S(1)}, bf16[28,16,128]{2,1,0:T(8,128)(2,1)S(1)}, u32[]{:S(2)}, u32[]{:S(2)}) %collective-permute-start.23) | collective-permute-done | bytes 114720 | tf_op jit(solution)/shard_map/ppermute | solution.py:38
  105.4 3.8 %collective-permute-done.24 = bf16[56,16,128]{2,1,0:T(8,128)(2,1)S(1)} collective-permute-done((bf16[56,16,128]{2,1,0:T(8,128)(2,1)S(1)}, bf16[56,16,128]{2,1,0:T(8,128)(2,1)S(1)}, u32[]{:S(2)}, u32[]{:S(2)}) %collective-permute-start.24) | collective-permute-done | bytes 229408 | tf_op jit(solution)/shard_map/ppermute | solution.py:38
  111.7 2.4 %assemble.1 = (f32[128,5376]{1,0:T(8,128)}, f32[128,1024]{1,0:T(8,128)}) custom-call(s32[3]{0:T(128)S(1)} %pad_add_fusion.1.scalars_ref, bf16[16,7,16,128]{3,2,1,0:T(8,128)(2,1)S(1)} %bitcast.41, bf16[16,6,16,128]{3,2,1,0:T(8,128)(2,1)S(1)} %bitcast.42, bf16[16,7,16,128]{3,2,1,0:T(8,128)(2,1)S(1)} %bitcast.44, bf16[16,6,16,128]{3,2,1,0:T(8,128)(2,1)S(1)} %bitcast.45), custom_call_target="tpu_custom_call" | custom-call | tf_op jit(solution)/shard_map/assemble/pallas_call | solution.py:697
  (78 shorter events, 35.2 us)
Async XLA Ops:
  0.6 35.2 %collective-permute-start.2 = (bf16[1,256,2048]{2,1,0:T(8,128)(2,1)}, bf16[1,256,2048]{2,1,0:T(8,128)(2,1)S(1)}, u32[]{:S(2)}, u32[]{:S(2)}) collective-permute-start(bf16[1,256,2048]{2,1,0:T(8,128)(2,1)} %param.14), channel_id=1, source_target_pairs={{0,16},{16,0},{1,17},{17,1},{2,18},{18,2},{3,19},{19,3},{4,20},{20... | collective-permute-start | bytes 3145736 | tf_op jit(solution)/shard_map/ppermute | solution.py:33
  5.1 12.7 %collective-permute-start.3 = (bf16[256,640]{1,0:T(8,128)(2,1)S(1)}, bf16[256,640]{1,0:T(8,128)(2,1)S(1)}, u32[]{:S(2)}, u32[]{:S(2)}) collective-permute-start(bf16[256,640]{1,0:T(8,128)(2,1)S(1)} %get-tuple-element.41.a_ref.refs_2_), channel_id=1, source_target_pairs={{0,4},{2,6},{4,8},{6,10},{8,12},{10,14},{1,5},{3,7},{5,9},{7,11},{... | collective-permute-start | bytes 983048 | tf_op jit(solution)/shard_map/ppermute | solution.py:28
  9.8 14.1 %collective-permute-start.7 = (bf16[256,512]{1,0:T(8,128)(2,1)S(1)}, bf16[256,512]{1,0:T(8,128)(2,1)S(1)}, u32[]{:S(2)}, u32[]{:S(2)}) collective-permute-start(bf16[256,512]{1,0:T(8,128)(2,1)S(1)} %get-tuple-element.44.a_ref.refs_2_), channel_id=1, source_target_pairs={{0,4},{2,6},{4,8},{6,10},{8,12},{10,14},{1,5},{3,7},{5,9},{7,11},{... | collective-permute-start | bytes 786440 | tf_op jit(solution)/shard_map/ppermute | solution.py:28
  13.2 15.8 %collective-permute-start.5 = (bf16[256,512]{1,0:T(8,128)(2,1)S(1)}, bf16[256,512]{1,0:T(8,128)(2,1)S(1)}, u32[]{:S(2)}, u32[]{:S(2)}) collective-permute-start(bf16[256,512]{1,0:T(8,128)(2,1)S(1)} %get-tuple-element.43.a_ref.refs_2_), channel_id=1, source_target_pairs={{0,4},{2,6},{4,8},{6,10},{8,12},{10,14},{1,5},{3,7},{5,9},{7,11},{... | collective-permute-start | bytes 786440 | tf_op jit(solution)/shard_map/ppermute | solution.py:28
  17.9 17.9 %collective-permute-start.4 = (bf16[256,640]{1,0:T(8,128)(2,1)S(1)}, bf16[256,640]{1,0:T(8,128)(2,1)S(1)}, u32[]{:S(2)}, u32[]{:S(2)}) collective-permute-start(bf16[256,640]{1,0:T(8,128)(2,1)S(1)} %choose.5), channel_id=1, source_target_pairs={{0,2},{2,0},{4,6},{6,4},{8,10},{10,8},{12,14},{14,12},{1,3},{3,1},... | collective-permute-start | bytes 983048 | tf_op jit(solution)/shard_map/ppermute | solution.py:38
  19.4 14.8 %collective-permute-start = (bf16[256,512]{1,0:T(8,128)(2,1)S(1)}, bf16[256,512]{1,0:T(8,128)(2,1)S(1)}, u32[]{:S(2)}, u32[]{:S(2)}) collective-permute-start(bf16[256,512]{1,0:T(8,128)(2,1)S(1)} %get-tuple-element.35.a_ref.refs_2_), channel_id=1, source_target_pairs={{0,4},{2,6},{4,8},{6,10},{8,12},{10,14},{1,5},{3,7},{5,9},{7,11},{... | collective-permute-start | bytes 786440 | tf_op jit(solution)/shard_map/ppermute | solution.py:28
  23.9 16.4 %collective-permute-start.8 = (bf16[256,512]{1,0:T(8,128)(2,1)S(1)}, bf16[256,512]{1,0:T(8,128)(2,1)S(1)}, u32[]{:S(2)}, u32[]{:S(2)}) collective-permute-start(bf16[256,512]{1,0:T(8,128)(2,1)S(1)} %choose.7), channel_id=1, source_target_pairs={{0,2},{2,0},{4,6},{6,4},{8,10},{10,8},{12,14},{14,12},{1,3},{3,1},... | collective-permute-start | bytes 786440 | tf_op jit(solution)/shard_map/ppermute | solution.py:38
  29.1 15.0 %collective-permute-start.6 = (bf16[256,512]{1,0:T(8,128)(2,1)S(1)}, bf16[256,512]{1,0:T(8,128)(2,1)S(1)}, u32[]{:S(2)}, u32[]{:S(2)}) collective-permute-start(bf16[256,512]{1,0:T(8,128)(2,1)S(1)} %choose.6), channel_id=1, source_target_pairs={{0,2},{2,0},{4,6},{6,4},{8,10},{10,8},{12,14},{14,12},{1,3},{3,1},... | collective-permute-start | bytes 786440 | tf_op jit(solution)/shard_map/ppermute | solution.py:38
  34.2 14.0 %collective-permute-start.1 = (bf16[256,512]{1,0:T(8,128)(2,1)S(1)}, bf16[256,512]{1,0:T(8,128)(2,1)S(1)}, u32[]{:S(2)}, u32[]{:S(2)}) collective-permute-start(bf16[256,512]{1,0:T(8,128)(2,1)S(1)} %choose.4), channel_id=1, source_target_pairs={{0,2},{2,0},{4,6},{6,4},{8,10},{10,8},{12,14},{14,12},{1,3},{3,1},... | collective-permute-start | bytes 786440 | tf_op jit(solution)/shard_map/ppermute | solution.py:38
  52.2 8.1 %collective-permute-start.11 = (bf16[256,2048]{1,0:T(8,128)(2,1)S(1)}, bf16[256,2048]{1,0:T(8,128)(2,1)S(1)}, u32[]{:S(2)}, u32[]{:S(2)}) collective-permute-start(bf16[256,2048]{1,0:T(8,128)(2,1)S(1)} %get-tuple-element.59), channel_id=1, source_target_pairs={{0,16},{16,0},{1,17},{17,1},{2,18},{18,2},{3,19},{19,3},{4,20},{20... | collective-permute-start | bytes 3145736 | tf_op jit(solution)/shard_map/ppermute | solution.py:33
  52.2 5.6 %collective-permute-start.10 = (bf16[32,256]{1,0:T(8,128)(2,1)S(1)}, bf16[32,256]{1,0:T(8,128)(2,1)S(1)}, u32[]{:S(2)}, u32[]{:S(2)}) collective-permute-start(bf16[32,256]{1,0:T(8,128)(2,1)S(1)} %get-tuple-element.56), channel_id=1, source_target_pairs={{2,0},{4,2},{6,4},{8,6},{10,8},{12,10},{14,12},{3,1},{5,3},{7,5},{... | collective-permute-start | bytes 49160 | tf_op jit(solution)/shard_map/ppermute | solution.py:28
  53.5 6.7 %collective-permute-start.9 = (bf16[32,256]{1,0:T(8,128)(2,1)S(1)}, bf16[32,256]{1,0:T(8,128)(2,1)S(1)}, u32[]{:S(2)}, u32[]{:S(2)}) collective-permute-start(bf16[32,256]{1,0:T(8,128)(2,1)S(1)} %get-tuple-element.55), channel_id=1, source_target_pairs={{4,0},{6,2},{8,4},{10,6},{12,8},{14,10},{5,1},{7,3},{9,5},{11,7},{... | collective-permute-start | bytes 49160 | tf_op jit(solution)/shard_map/ppermute | solution.py:28
  65.5 7.0 %collective-permute-start.15 = (bf16[48,16,128]{2,1,0:T(8,128)(2,1)S(1)}, bf16[48,16,128]{2,1,0:T(8,128)(2,1)S(1)}, u32[]{:S(2)}, u32[]{:S(2)}) collective-permute-start(bf16[48,16,128]{2,1,0:T(8,128)(2,1)S(1)} %constant_dynamic-slice_fusion.1), channel_id=1, source_target_pairs={{0,1},{1,0},{2,3},{3,2},{4,5},{5,4},{6,7},{7,6},{8,9},{9,8},{10,11... | collective-permute-start | bytes 589832 | tf_op jit(solution)/shard_map/ppermute | solution.py:38
  67.1 7.7 %collective-permute-start.13 = (bf16[56,16,128]{2,1,0:T(8,128)(2,1)S(1)}, bf16[56,16,128]{2,1,0:T(8,128)(2,1)S(1)}, u32[]{:S(2)}, u32[]{:S(2)}) collective-permute-start(bf16[56,16,128]{2,1,0:T(8,128)(2,1)S(1)} %constant_dynamic-slice_fusion.3), channel_id=1, source_target_pairs={{0,2},{2,0},{4,6},{6,4},{8,10},{10,8},{12,14},{14,12},{1,3},{3,1},... | collective-permute-start | bytes 688136 | tf_op jit(solution)/shard_map/ppermute | solution.py:38
  74.9 4.9 %collective-permute-start.14 = (bf16[28,16,128]{2,1,0:T(8,128)(2,1)S(1)}, bf16[28,16,128]{2,1,0:T(8,128)(2,1)S(1)}, u32[]{:S(2)}, u32[]{:S(2)}) collective-permute-start(bf16[28,16,128]{2,1,0:T(8,128)(2,1)S(1)} %constant_dynamic-slice_fusion.2), channel_id=1, source_target_pairs={{0,1},{1,0},{2,3},{3,2},{4,5},{5,4},{6,7},{7,6},{8,9},{9,8},{10,11... | collective-permute-start | bytes 344072 | tf_op jit(solution)/shard_map/ppermute | solution.py:38
  79.8 4.7 %collective-permute-start.17 = (bf16[1,13,16,128]{3,2,1,0:T(8,128)(2,1)S(1)}, bf16[1,13,16,128]{3,2,1,0:T(8,128)(2,1)S(1)}, u32[]{:S(2)}, u32[]{:S(2)}) collective-permute-start(bf16[1,13,16,128]{3,2,1,0:T(8,128)(2,1)S(1)} %get-tuple-element.67), channel_id=1, source_target_pairs={{0,4},{2,6},{4,0},{6,2},{8,12},{10,14},{12,8},{14,10},{1,5},{3,7},... | collective-permute-start | bytes 159752 | tf_op jit(solution)/shard_map/ppermute | solution.py:38
  81.9 5.6 %collective-permute-start.18 = (bf16[1,13,16,128]{3,2,1,0:T(8,128)(2,1)S(1)}, bf16[1,13,16,128]{3,2,1,0:T(8,128)(2,1)S(1)}, u32[]{:S(2)}, u32[]{:S(2)}) collective-permute-start(bf16[1,13,16,128]{3,2,1,0:T(8,128)(2,1)S(1)} %get-tuple-element.68), channel_id=1, source_target_pairs={{0,8},{2,10},{4,12},{6,14},{8,0},{10,2},{12,4},{14,6},{1,9},{3,11}... | collective-permute-start | bytes 159752 | tf_op jit(solution)/shard_map/ppermute | solution.py:38
  83.2 6.0 %collective-permute-start.19 = (bf16[1,13,16,128]{3,2,1,0:T(8,128)(2,1)S(1)}, bf16[1,13,16,128]{3,2,1,0:T(8,128)(2,1)S(1)}, u32[]{:S(2)}, u32[]{:S(2)}) collective-permute-start(bf16[1,13,16,128]{3,2,1,0:T(8,128)(2,1)S(1)} %get-tuple-element.69), channel_id=1, source_target_pairs={{0,12},{2,14},{4,8},{6,10},{8,4},{10,6},{12,0},{14,2},{1,13},{3,15... | collective-permute-start | bytes 159752 | tf_op jit(solution)/shard_map/ppermute | solution.py:38
  90.0 5.0 %collective-permute-start.21 = (bf16[1,13,16,128]{3,2,1,0:T(8,128)(2,1)S(1)}, bf16[1,13,16,128]{3,2,1,0:T(8,128)(2,1)S(1)}, u32[]{:S(2)}, u32[]{:S(2)}) collective-permute-start(bf16[1,13,16,128]{3,2,1,0:T(8,128)(2,1)S(1)} %add_convert_fusion.4), channel_id=1, source_target_pairs={{0,8},{2,10},{4,12},{6,14},{8,0},{10,2},{12,4},{14,6},{1,9},{3,11}... | collective-permute-start | bytes 159752 | tf_op jit(solution)/shard_map/ppermute | solution.py:38
  91.3 5.9 %collective-permute-start.22 = (bf16[1,13,16,128]{3,2,1,0:T(8,128)(2,1)S(1)}, bf16[1,13,16,128]{3,2,1,0:T(8,128)(2,1)S(1)}, u32[]{:S(2)}, u32[]{:S(2)}) collective-permute-start(bf16[1,13,16,128]{3,2,1,0:T(8,128)(2,1)S(1)} %add_convert_fusion.4), channel_id=1, source_target_pairs={{0,12},{2,14},{4,8},{6,10},{8,4},{10,6},{12,0},{14,2},{1,13},{3,15... | collective-permute-start | bytes 159752 | tf_op jit(solution)/shard_map/ppermute | solution.py:38
  97.3 5.8 %collective-permute-start.23 = (bf16[28,16,128]{2,1,0:T(8,128)(2,1)S(1)}, bf16[28,16,128]{2,1,0:T(8,128)(2,1)S(1)}, u32[]{:S(2)}, u32[]{:S(2)}) collective-permute-start(bf16[28,16,128]{2,1,0:T(8,128)(2,1)S(1)} %bitcast.53), channel_id=1, source_target_pairs={{0,1},{1,0},{2,3},{3,2},{4,5},{5,4},{6,7},{7,6},{8,9},{9,8},{10,11... | collective-permute-start | bytes 344072 | tf_op jit(solution)/shard_map/ppermute | solution.py:38
  98.6 5.2 %collective-permute-start.25 = (bf16[24,16,128]{2,1,0:T(8,128)(2,1)S(1)}, bf16[24,16,128]{2,1,0:T(8,128)(2,1)S(1)}, u32[]{:S(2)}, u32[]{:S(2)}) collective-permute-start(bf16[24,16,128]{2,1,0:T(8,128)(2,1)S(1)} %bitcast.58), channel_id=1, source_target_pairs={{0,2},{2,0},{4,6},{6,4},{8,10},{10,8},{12,14},{14,12},{1,3},{3,1},... | collective-permute-start | bytes 294920 | tf_op jit(solution)/shard_map/ppermute | solution.py:38
  103.2 6.1 %collective-permute-start.24 = (bf16[56,16,128]{2,1,0:T(8,128)(2,1)S(1)}, bf16[56,16,128]{2,1,0:T(8,128)(2,1)S(1)}, u32[]{:S(2)}, u32[]{:S(2)}) collective-permute-start(bf16[56,16,128]{2,1,0:T(8,128)(2,1)S(1)} %pad_maximum_fusion.2), channel_id=1, source_target_pairs={{0,2},{2,0},{4,6},{6,4},{8,10},{10,8},{12,14},{14,12},{1,3},{3,1},... | collective-permute-start | bytes 688136 | tf_op jit(solution)/shard_map/ppermute | solution.py:38
  103.8 5.7 %collective-permute-start.26 = (bf16[48,16,128]{2,1,0:T(8,128)(2,1)S(1)}, bf16[48,16,128]{2,1,0:T(8,128)(2,1)S(1)}, u32[]{:S(2)}, u32[]{:S(2)}) collective-permute-start(bf16[48,16,128]{2,1,0:T(8,128)(2,1)S(1)} %pad_maximum_fusion.3), channel_id=1, source_target_pairs={{0,1},{1,0},{2,3},{3,2},{4,5},{5,4},{6,7},{7,6},{8,9},{9,8},{10,11... | collective-permute-start | bytes 589832 | tf_op jit(solution)/shard_map/ppermute | solution.py:38
  (11 other events, 168.6 us)
where the time goes:
time: 115 us; the launch traced here: 114 us
  starting transfers between devices  46.4 us (40%)
  waiting for transfers between devices  37.5 us (33%)
  Pallas kernels  27.6 us (24%)
    ppermute x18, starting transfers between devices, permute_xor(): return lax.ppermute(value, axis, [(i, i ^ bit) for i in range(count)])  26.6 us
    ppermute x18, waiting for transfers between devices, permute_xor(): return lax.ppermute(value, axis, [(i, i ^ bit) for i in range(count)])  22.7 us
    ppermute x6, starting transfers between devices, permute_by(): lax.ppermute(value, axis, [(i, i + steps) for i in range(first, last)])  18.6 us
    pallas_call x4, Pallas kernels, attention(): pl.pallas_call(partial(attention_kernel, n_blocks=n_blocks, first_head=fi...  15.3 us
    ppermute x6, waiting for transfers between devices, permute_by(): lax.ppermute(value, axis, [(i, i + steps) for i in range(first, last)])  10.8 us
    ppermute x5, waiting for transfers between devices, permute_cyclic(): lax.ppermute(value, axis, [(i, (i + by) % count) for i in range(count)])  4.05 us
    pallas_call x1, Pallas kernels, pack(): pl.pallas_call(partial(pack_kernel, pieces=pieces, lanes=lanes), in_specs...  3.8 us
    pallas_call x1, Pallas kernels, tables(): pl.pallas_call(partial(tables_kernel, adapters=adapters, rank=rank), in_s...  3.22 us
  transfers between devices with their start and end apart: 29, of which 18 were waited for; matrix products, arithmetic and copies ran while one was open for 0% of the time, Pallas kernels for 16%

commit v1 on v0

--- a/solution.py
+++ b/solution.py
@@ -473,46 +473,58 @@
     handing.wait()
 
 
-def merge_kernel(keep_ref, recv_ref, *out_refs):
-    at = 0
-    for ref in out_refs:
-        rows = slice(at, at + ref.shape[0])
-        ref[...] = (keep_ref[rows].astype(f32) + recv_ref[rows].astype(f32)).astype(bf16)
-        at += ref.shape[0]
-
-
-def assemble_kernel(
-    scalars_ref, ma_ref, mb_ref, ra_ref, rb_ref, w_hbm, u_hbm, w_ref, u_ref, sems, *, cols, rows
-):
-    side, me_a, me_b = scalars_ref[0], scalars_ref[1], scalars_ref[2]
-    n_a, a = ma_ref.shape[:2]
-    b = mb_ref.shape[1]
+def merge_kernel(keep_ref, recv_ref, out_ref):
+    out_ref[...] = (keep_ref[...].astype(f32) + recv_ref[...].astype(f32)).astype(bf16)
+
+
+def assemble_kernel(scalars_ref, tiles_ref, *refs, cols, rows, own):
+    w_hbm, u_hbm, w_ref, u_ref, sems = refs[-5:]
+    side, me = scalars_ref[0], scalars_ref[1]
+    half = side if own else 1 - side
+    units = tiles_ref.shape[1]
     up_cols = u_ref.shape[1] // HD
     per_row = cols + up_cols
     stores = []
     for r in range(rows):
-        starts = [pl.multiple_of((m * rows + r) * SUB, SUB) for m in (side, 1 - side)]
+        at = slice(r * SUB, (r + 1) * SUB)
         for c in range(per_row):
             t = r * per_row + c
-            if t < n_a * a:
-                mine, theirs, piece, off = ma_ref, ra_ref, (t // a) ^ me_a, t % a
+            tile = tiles_ref[(t // units) ^ me, t % units].astype(f32)
+            if c < cols:
+                w_ref[at, c * HD : (c + 1) * HD] = tile
             else:
-                t -= n_a * a
-                mine, theirs, piece, off = mb_ref, rb_ref, (t // b) ^ me_b, t % b
-            for src, at in zip((mine, theirs), starts):
-                tile = src[piece, off].astype(f32)
-                if c < cols:
-                    w_ref[pl.ds(at, SUB), c * HD : (c + 1) * HD] = tile
-                else:
-                    u_ref[pl.ds(at, SUB), (c - cols) * HD : (c - cols + 1) * HD] = tile
-        for at in starts:
-            band = pl.ds(at, SUB)
-            stores.append(pltpu.make_async_copy(w_ref.at[band], w_hbm.at[band], sems.at[len(stores)]))
+                u_ref[at, (c - cols) * HD : (c - cols + 1) * HD] = tile
+        band = pl.ds(pl.multiple_of((half * rows + r) * SUB, SUB), SUB)
+        for src, dst in ((w_ref, w_hbm), (u_ref, u_hbm)):
+            stores.append(pltpu.make_async_copy(src.at[at], dst.at[band], sems.at[len(stores)]))
             stores[-1].start()
-    stores.append(pltpu.make_async_copy(u_ref, u_hbm, sems.at[len(stores)]))
-    stores[-1].start()
     for store in stores:
         store.wait()
+
+
+def assemble(scalars, tiles, before, width, model_width, kv_width):
+    rows = width // 2 // SUB
+    hbm = pl.BlockSpec(memory_space=pltpu.HBM)
+    carried = [] if before is None else [in_hbm(x) for x in before]
+    shapes = [(width, model_width), (width, kv_width)]
+    return pl.pallas_call(
+        partial(assemble_kernel, cols=model_width // HD, rows=rows, own=before is None),
+        in_specs=[
+            pl.BlockSpec(memory_space=pltpu.SMEM),
+            pl.BlockSpec(memory_space=pltpu.VMEM),
+            *[hbm for _ in carried],
+        ],
+        out_specs=[hbm, hbm],
+        out_shape=[jax.ShapeDtypeStruct(shape, f32) for shape in shapes],
+        scratch_shapes=[
+            pltpu.VMEM((width // 2, model_width), f32),
+            pltpu.VMEM((width // 2, kv_width), f32),
+            pltpu.SemaphoreType.DMA((2 * rows,)),
+        ],
+        input_output_aliases={2 + i: i for i in range(len(carried))},
+        compiler_params=pltpu.CompilerParams(vmem_limit_bytes=16 << 20),
+        name="assemble",
+    )(scalars, in_vmem(tiles), *carried)
 
 
 def axis_bits(axis):
@@ -528,41 +540,38 @@
     return ((lax.axis_index(axis) & bit) != 0).astype(jnp.int32)
 
 
-def direct_peers(axis, bits):
-    masks = [0]
-    for bit in bits:
-        masks = masks + [m | bit for m in masks]
+def permute_masked(value, masks):
+    axes = tuple(masks)
+    sizes = [lax.axis_size(axis) for axis in axes]
+    pairs = []
+    for i in range(int(np.prod(sizes))):
+        index = np.unravel_index(i, sizes)
+        pairs.append((i, int(np.ravel_multi_index([k ^ masks[x] for k, x in zip(index, axes)], sizes))))
+    return lax.ppermute(value, axes if len(axes) > 1 else axes[0], pairs)
+
+
+def direct_peers(stages):
+    masks = [{axis: 0 for axis, _ in stages}]
+    for axis, bit in stages:
+        masks = masks + [{**m, axis: m[axis] | bit} for m in masks]
     me = jnp.int32(0)
-    for bit in reversed(bits):
-        me = me * 2 + bit_of((axis, bit))
+    for stage in reversed(stages):
+        me = me * 2 + bit_of(stage)
     return masks, me
 
 
-def direct_scatter(tiles, axis, bits):
-    masks, me = direct_peers(axis, bits)
+def direct_scatter(tiles, stages):
+    masks, me = direct_peers(stages)
     total = lax.dynamic_index_in_dim(tiles, me, 0, keepdims=False).astype(f32)
     for j in range(1, len(masks)):
         part = lax.dynamic_index_in_dim(tiles, me ^ j, 0, keepdims=False)
-        total = total + permute_xor(part, axis, masks[j]).astype(f32)
+        total = total + permute_masked(part, masks[j]).astype(f32)
     return total.astype(bf16)
 
 
-def direct_gather(tiles, axis, bits):
-    masks, _ = direct_peers(axis, bits)
-    return jnp.stack([tiles] + [permute_xor(tiles, axis, m) for m in masks[1:]])
-
-
-def scatter_stage(tiles, stage):
-    n = tiles.shape[0] // 2
-    bit = bit_of(stage)
-    send = lax.dynamic_slice_in_dim(tiles, (1 - bit) * n, n, 0)
-    keep = lax.dynamic_slice_in_dim(tiles, bit * n, n, 0)
-    recv = permute_xor(send, *stage)
-    return (keep.astype(f32) + recv.astype(f32)).astype(bf16)
-
-
-def gather_stage(tiles, stage):
-    return jnp.concatenate([tiles, permute_xor(tiles, *stage)], axis=0)
+def direct_gather(tiles, stages):
+    masks, _ = direct_peers(stages)
+    return jnp.stack([tiles] + [permute_masked(tiles, m) for m in masks[1:]])
 
 
 def step(
@@ -621,16 +630,12 @@
     received = [permute_by(low, "ctx", j - 2 * steps) for j, low in enumerate(lows[:-1])]
     handed = permute_cyclic(out, "section", 1)[None]
 
-    other = (
-        axis_bits("ctx")[:1] + axis_bits("dp"),
-        axis_bits("dp") + axis_bits("ctx")[:1],
-    )
-    tail = [bit for _, bit in axis_bits("ctx")[1:]]
+    rest = axis_bits("ctx")[1:]
+    rounds = [axis_bits("ctx")[:1] + axis_bits("dp")]
+    rounds += [rest[k : k + 2] for k in range(0, len(rest), 2)]
     group = lax.axis_size("ctx") * lax.axis_size("dp")
     cols, up_cols, rows = model_width // HD, kv_heads, half // SUB
     units = -(-(rows * (cols + up_cols)) // group)
-    a = (units + 1) // 2
-    b = units - a
     side = lax.axis_index("section").astype(jnp.int32)
     smem = pl.BlockSpec(memory_space=pltpu.SMEM)
     vmem = pl.BlockSpec(memory_space=pltpu.VMEM)
@@ -658,64 +663,27 @@
         in_hbm(hidden[0]),
     )
     recv = permute_cyclic(send, "section", 1)
-    colours = pl.pallas_call(
+    tiles = pl.pallas_call(
         merge_kernel,
         in_specs=[vmem, vmem],
-        out_specs=[vmem, vmem],
-        out_shape=[pltpu.VMEM((n * group, SUB, HD), bf16) for n in (a, b)],
+        out_specs=vmem,
+        out_shape=pltpu.VMEM(tile_shape, bf16),
         compiler_params=pltpu.CompilerParams(vmem_limit_bytes=8 << 20),
         name="merge",
     )(in_vmem(keep), in_vmem(recv))
-    for k in range(len(other[0])):
-        colours = [scatter_stage(colours[c], other[c][k]) for c in range(2)]
-    rounds = [tail[k : k + 2] for k in range(0, len(tail), 2)]
-    members = group >> len(other[0])
-    joined = jnp.concatenate([c.reshape(members, -1, SUB, HD) for c in colours], axis=1)
-    for bits in rounds:
-        joined = joined.reshape(2 ** len(bits), -1, a + b, SUB, HD)
-        joined = direct_scatter(joined, "ctx", bits)
-    joined = joined.reshape(a + b, SUB, HD)
-    ids = []
-    for c in range(2):
-        me = jnp.int32(0)
-        for stage in other[c]:
-            me = me * 2 + bit_of(stage)
-        for bits in rounds:
-            me = me * 2 ** len(bits) + direct_peers("ctx", bits)[1]
-        ids.append(me)
-    joined = joined[None]
-    for bits in reversed(rounds):
-        joined = direct_gather(joined, "ctx", bits).reshape(-1, a + b, SUB, HD)
-    colours = [
-        joined[:, :a].reshape(-1, SUB, HD),
-        joined[:, a:].reshape(-1, SUB, HD),
-    ]
-    for k in reversed(range(len(other[0]))):
-        colours = [gather_stage(colours[c], other[c][k]) for c in range(2)]
-    theirs = [permute_cyclic(t, "section", 1) for t in colours]
-    shapes = [(group, a, SUB, HD), (group, b, SUB, HD)]
-    w, u = pl.pallas_call(
-        partial(assemble_kernel, cols=cols, rows=rows),
-        in_specs=[smem] + [vmem] * 4,
-        out_specs=[any_space, any_space],
-        out_shape=[
-            jax.ShapeDtypeStruct((width, model_width), f32),
-            jax.ShapeDtypeStruct((width, kv_width), f32),
-        ],
-        scratch_shapes=[
-            pltpu.VMEM((width, model_width), f32),
-            pltpu.VMEM((width, kv_width), f32),
-            pltpu.SemaphoreType.DMA((2 * rows + 1,)),
-        ],
-        compiler_params=pltpu.CompilerParams(vmem_limit_bytes=16 << 20),
-        name="assemble",
-    )(
-        jnp.stack([side, ids[0], ids[1]]),
-        in_vmem(colours[0].reshape(shapes[0])),
-        in_vmem(colours[1].reshape(shapes[1])),
-        in_vmem(theirs[0].reshape(shapes[0])),
-        in_vmem(theirs[1].reshape(shapes[1])),
-    )
+    me = jnp.int32(0)
+    for stages in rounds:
+        tiles = direct_scatter(tiles.reshape(2 ** len(stages), -1, SUB, HD), stages)
+        me = me * 2 ** len(stages) + direct_peers(stages)[1]
+    for stages in reversed(rounds):
+        tiles = direct_gather(tiles, stages).reshape(-1, SUB, HD)
+    theirs = permute_cyclic(tiles, "section", 1)
+    scalars = jnp.stack([side, me])
+    outs = None
+    for part in (tiles, theirs):
+        part = part.reshape(group, units, SUB, HD)
+        outs = assemble(scalars, part, outs, width, model_width, kv_width)
+    w, u = outs
     down_map_gradient = w.T.reshape(model_width, 2, adapters, rank)
     up_map_gradient = u.reshape(2, adapters, rank, kv_width)
     return (handed, down_map_gradient, up_map_gradient)

time: 115 us -> 112 us (0.974)
  starting transfers between devices: 46.4 us -> 41.4 us
  Pallas kernels: 27.6 us -> 28.8 us
    ppermute x0 -> x12, waiting for transfers between devices: none -> 24.8 us  [permute_masked(): return lax.ppermute(value, axes if len(axes) > 1 else axes[0], pairs)]
    ppermute x18 -> x4, waiting for transfers between devices: 22.7 us -> 0.01 us  [permute_xor(): return lax.ppermute(value, axis, [(i, i ^ bit) for i in range(count)])]
    ppermute x18 -> x4, starting transfers between devices: 26.6 us -> 5.83 us  [permute_xor(): return lax.ppermute(value, axis, [(i, i ^ bit) for i in range(count)])]
    ppermute x0 -> x12, starting transfers between devices: none -> 16.2 us  [permute_masked(): return lax.ppermute(value, axes if len(axes) > 1 else axes[0], pairs)]
    ppermute x5 -> x4, waiting for transfers between devices: 4.05 us -> 2.84 us  [permute_cyclic(): lax.ppermute(value, axis, [(i, (i + by) % count) for i in range(count)])]
    pallas_call x2 -> x3, Pallas kernels: 2.56 us -> 3.76 us  [the longest x2 3.57 us: assemble(): pl.pallas_call(partial(assemble_kernel, cols=model_width // HD, rows=rows...]
  transfers between devices with their start and end apart: 29 -> 26, of which waited for: 18 -> 16; matrix products, arithmetic and copies ran while one was open for 0% -> 0% of each run, Pallas kernels for 16% -> 18%
where the time goes in v1:
time: 112 us; the launch traced here: 111 us
  starting transfers between devices  41.4 us (37%)
  waiting for transfers between devices  38.4 us (34%)
  Pallas kernels  28.8 us (26%)
  local copies, waits for them, and re-layouts  1.14 us (1%)
    ppermute x12, waiting for transfers between devices, permute_masked(): return lax.ppermute(value, axes if len(axes) > 1 else axes[0], pairs)  24.8 us
    ppermute x6, starting transfers between devices, permute_by(): lax.ppermute(value, axis, [(i, i + steps) for i in range(first, last)])  18.6 us
    ppermute x12, starting transfers between devices, permute_masked(): return lax.ppermute(value, axes if len(axes) > 1 else axes[0], pairs)  16.2 us
    pallas_call x4, Pallas kernels, attention(): pl.pallas_call(partial(attention_kernel, n_blocks=n_blocks, first_head=fi...  15.3 us
    ppermute x6, waiting for transfers between devices, permute_by(): lax.ppermute(value, axis, [(i, i + steps) for i in range(first, last)])  10.8 us
    ppermute x4, starting transfers between devices, permute_xor(): return lax.ppermute(value, axis, [(i, i ^ bit) for i in range(count)])  5.83 us
    pallas_call x1, Pallas kernels, pack(): pl.pallas_call(partial(pack_kernel, pieces=pieces, lanes=lanes), in_specs...  3.8 us
    pallas_call x2, Pallas kernels, assemble(): pl.pallas_call(partial(assemble_kernel, cols=model_width // HD, rows=rows...  3.57 us
  transfers between devices with their start and end apart: 26, of which 16 were waited for; matrix products, arithmetic and copies ran while one was open for 0% of the time, Pallas kernels for 18%

profile of v1, /device:TPU:0, one launch (start us, length us, event | category | flops | bytes accessed | tf_op | source)
XLA Modules:
  0.0 111.3 jit_solution(1694147225402035631)
XLA Ops:
  1.3 3.8 %pack.1 = (bf16[256,640]{1,0:T(8,128)(2,1)S(1)}, bf16[256,512]{1,0:T(8,128)(2,1)S(1)}, bf16[256,512]{1,0:T(8,128)(2,1)S(1)}, bf16[256,512]{1,0:T(8,128)(2,1)S(1)}, s32[2]{0:T(128)S(4)}) custom-call(s32[2]{0:T(128)S(1)} %pad_add_fusion.place_ref, bf16[256,5376]{1,0:T(8,128)(2,1)} %bitcast.68, bf16[128,5376]{1,0:T(8,128)(2,1)} %bitcast.71, ...), custom_call_target="tpu_custom_call" | custom-call | tf_op jit(solution)/shard_map/pack/pallas_call | solution.py:187
  5.1 4.6 %collective-permute-start.3 = (bf16[256,640]{1,0:T(8,128)(2,1)S(1)}, bf16[256,640]{1,0:T(8,128)(2,1)S(1)}, u32[]{:S(2)}, u32[]{:S(2)}) collective-permute-start(bf16[256,640]{1,0:T(8,128)(2,1)S(1)} %get-tuple-element.41.a_ref.refs_2_), channel_id=1, source_target_pairs={{0,4},{2,6},{4,8},{6,10},{8,12},{10,14},{1,5},{3,7},{5,9},{7,11},{... | collective-permute-start | bytes 983048 | tf_op jit(solution)/shard_map/ppermute | solution.py:28
  9.8 3.5 %collective-permute-start.7 = (bf16[256,512]{1,0:T(8,128)(2,1)S(1)}, bf16[256,512]{1,0:T(8,128)(2,1)S(1)}, u32[]{:S(2)}, u32[]{:S(2)}) collective-permute-start(bf16[256,512]{1,0:T(8,128)(2,1)S(1)} %get-tuple-element.44.a_ref.refs_2_), channel_id=1, source_target_pairs={{0,4},{2,6},{4,8},{6,10},{8,12},{10,14},{1,5},{3,7},{5,9},{7,11},{... | collective-permute-start | bytes 786440 | tf_op jit(solution)/shard_map/ppermute | solution.py:28
  13.2 3.5 %collective-permute-start.5 = (bf16[256,512]{1,0:T(8,128)(2,1)S(1)}, bf16[256,512]{1,0:T(8,128)(2,1)S(1)}, u32[]{:S(2)}, u32[]{:S(2)}) collective-permute-start(bf16[256,512]{1,0:T(8,128)(2,1)S(1)} %get-tuple-element.43.a_ref.refs_2_), channel_id=1, source_target_pairs={{0,4},{2,6},{4,8},{6,10},{8,12},{10,14},{1,5},{3,7},{5,9},{7,11},{... | collective-permute-start | bytes 786440 | tf_op jit(solution)/shard_map/ppermute | solution.py:28
  19.4 4.4 %collective-permute-start = (bf16[256,512]{1,0:T(8,128)(2,1)S(1)}, bf16[256,512]{1,0:T(8,128)(2,1)S(1)}, u32[]{:S(2)}, u32[]{:S(2)}) collective-permute-start(bf16[256,512]{1,0:T(8,128)(2,1)S(1)} %get-tuple-element.35.a_ref.refs_2_), channel_id=1, source_target_pairs={{0,4},{2,6},{4,8},{6,10},{8,12},{10,14},{1,5},{3,7},{5,9},{7,11},{... | collective-permute-start | bytes 786440 | tf_op jit(solution)/shard_map/ppermute | solution.py:28
  25.0 4.0 %collective-permute-done.5.b_ref.refs_0_ = bf16[256,512]{1,0:T(8,128)(2,1)S(1)} collective-permute-done((bf16[256,512]{1,0:T(8,128)(2,1)S(1)}, bf16[256,512]{1,0:T(8,128)(2,1)S(1)}, u32[]{:S(2)}, u32[]{:S(2)}) %collective-permute-start.5) | collective-permute-done | bytes 262176 | tf_op jit(solution)/shard_map/ppermute | solution.py:28
  30.6 3.2 %tables.1 = (bf16[768,128]{1,0:T(8,128)(2,1)S(1)}, f32[128,256]{1,0:T(8,128)S(1)}, f32[768,256]{1,0:T(8,128)S(1)}, f32[768,128]{1,0:T(8,128)S(1)}, f32[768,128]{1,0:T(8,128)S(1)}) custom-call(s32[2]{0:T(128)S(4)} %get-tuple-element.36.second_ref.place_ref, s32[1,16]{1,0:T(1,128)S(1)} %copy-done.2, s32[1,16]{1,0:T(1,128)S(1)} %copy-done.3, f32[1,128]{1,0:T(1,128)S(1)} %copy-done.4), custom_call_target="tpu_custom_call" | custom-call | tf_op jit(solution)/shard_map/tables/pallas_call | solution.py:114
  36.8 3.5 %attention.4 = (bf16[256,2048]{1,0:T(8,128)(2,1)S(1)}, bf16[2,64,1024]{2,1,0:T(8,128)(2,1)S(1)}, f32[768,128]{1,0:T(8,128)S(1)}, bf16[768,128]{1,0:T(8,128)(2,1)S(1)}) custom-call(bf16[256,640]{1,0:T(8,128)(2,1)S(1)} %collective-permute-done.3.b_ref.refs_0_, bf16[256,640]{1,0:T(8,128)(2,1)S(1)} %collective-permute-done.4.refs_1_, ...), custom_call_target="tpu_custom_call" | custom-call | flops 1006632960 | bytes 1310720 | tf_op jit(solution)/shard_map/attention/pallas_call | solution.py:391
  40.2 3.9 %attention.5 = (bf16[256,2048]{1,0:T(8,128)(2,1)S(1)}, bf16[2,64,1024]{2,1,0:T(8,128)(2,1)S(1)}, f32[768,128]{1,0:T(8,128)S(1)}) custom-call(bf16[256,512]{1,0:T(8,128)(2,1)S(1)} %collective-permute-done.7.b_ref.refs_0_, bf16[256,512]{1,0:T(8,128)(2,1)S(1)} %collective-permute-done.8.refs_1_, ...), custom_call_target="tpu_custom_call", output_to_operand_aliasing={{0}: (12, {}), {1}: (13, {}), {2}: (11, {})} | custom-call | flops 1006632960 | bytes 1310720 | tf_op jit(solution)/shard_map/attention/pallas_call | solution.py:391
  44.1 4.1 %attention.6 = (bf16[256,2048]{1,0:T(8,128)(2,1)S(1)}, bf16[2,64,1024]{2,1,0:T(8,128)(2,1)S(1)}, f32[768,128]{1,0:T(8,128)S(1)}) custom-call(bf16[256,512]{1,0:T(8,128)(2,1)S(1)} %collective-permute-done.5.b_ref.refs_0_, bf16[256,512]{1,0:T(8,128)(2,1)S(1)} %collective-permute-done.6.refs_1_, ...), custom_call_target="tpu_custom_call", output_to_operand_aliasing={{0}: (12, {}), {1}: (13, {}), {2}: (11, {})} | custom-call | flops 1006632960 | bytes 1310720 | tf_op jit(solution)/shard_map/attention/pallas_call | solution.py:391
  48.2 4.0 %attention.7 = (bf16[256,2048]{1,0:T(8,128)(2,1)S(1)}, bf16[2,64,1024]{2,1,0:T(8,128)(2,1)S(1)}, bf16[32,256]{1,0:T(8,128)(2,1)S(1)}, bf16[32,256]{1,0:T(8,128)(2,1)S(1)}, bf16[32,256]{1,0:T(8,128)(2,1)S(1)}) custom-call(bf16[256,512]{1,0:T(8,128)(2,1)S(1)} %collective-permute-done.b_ref.refs_0_, ...), custom_call_target="tpu_custom_call", output_to_operand_aliasing={{0}: (12, {}), {1}: (13, {})} | custom-call | flops 1006632960 | bytes 1310720 | tf_op jit(solution)/shard_map/attention/pallas_call | solution.py:391
  54.8 3.0 %collective-permute-done.10.refs_3_ = bf16[32,256]{1,0:T(8,128)(2,1)S(1)} collective-permute-done((bf16[32,256]{1,0:T(8,128)(2,1)S(1)}, bf16[32,256]{1,0:T(8,128)(2,1)S(1)}, u32[]{:S(2)}, u32[]{:S(2)}) %collective-permute-start.10) | collective-permute-done | bytes 16416 | tf_op jit(solution)/shard_map/ppermute | solution.py:28
  57.9 2.4 %collective-permute-done.9.refs_2_ = bf16[32,256]{1,0:T(8,128)(2,1)S(1)} collective-permute-done((bf16[32,256]{1,0:T(8,128)(2,1)S(1)}, bf16[32,256]{1,0:T(8,128)(2,1)S(1)}, u32[]{:S(2)}, u32[]{:S(2)}) %collective-permute-start.9) | collective-permute-done | bytes 16416 | tf_op jit(solution)/shard_map/ppermute | solution.py:28
  60.2 2.6 %product.1 = (bf16[208,16,128]{2,1,0:T(8,128)(2,1)S(1)}, bf16[208,16,128]{2,1,0:T(8,128)(2,1)S(1)}, bf16[1,256,2048]{2,1,0:T(8,128)(2,1)}) custom-call(s32[1]{0:T(128)} %bitcast.refs_0_, bf16[32,256]{1,0:T(8,128)(2,1)S(1)} %get-tuple-element.54.refs_1_, bf16[32,256]{1,0:T(8,128)(2,1)S(1)} %collective-permute-done.9.refs_2_, ...), custom_call_target="tpu_custom_call" | custom-call | tf_op jit(solution)/shard_map/product/pallas_call | solution.py:645
  62.9 2.3 %collective-permute-done.12.recv_ref = bf16[208,16,128]{2,1,0:T(8,128)(2,1)S(1)} collective-permute-done((bf16[208,16,128]{2,1,0:T(8,128)(2,1)S(1)}, bf16[208,16,128]{2,1,0:T(8,128)(2,1)S(1)}, u32[]{:S(2)}, u32[]{:S(2)}) %collective-permute-start.12) | collective-permute-done | bytes 852000 | tf_op jit(solution)/shard_map/ppermute | solution.py:33
  65.6 2.1 %collective-permute-start.13 = (bf16[52,16,128]{2,1,0:T(8,128)(2,1)S(1)}, bf16[52,16,128]{2,1,0:T(8,128)(2,1)S(1)}, u32[]{:S(2)}, u32[]{:S(2)}) collective-permute-start(bf16[52,16,128]{2,1,0:T(8,128)(2,1)S(1)} %get-tuple-element.67), channel_id=1, source_target_pairs={{0,2},{1,3},{2,0},{3,1},{4,6},{5,7},{6,4},{7,5},{8,10},{9,11},{10,... | collective-permute-start | bytes 638984 | tf_op jit(solution)/shard_map/ppermute | solution.py:550
  69.2 4.6 %collective-permute-done.13 = bf16[52,16,128]{2,1,0:T(8,128)(2,1)S(1)} collective-permute-done((bf16[52,16,128]{2,1,0:T(8,128)(2,1)S(1)}, bf16[52,16,128]{2,1,0:T(8,128)(2,1)S(1)}, u32[]{:S(2)}, u32[]{:S(2)}) %collective-permute-start.13) | collective-permute-done | bytes 213024 | tf_op jit(solution)/shard_map/ppermute | solution.py:550
  73.8 5.5 %collective-permute-done.14 = bf16[52,16,128]{2,1,0:T(8,128)(2,1)S(1)} collective-permute-done((bf16[52,16,128]{2,1,0:T(8,128)(2,1)S(1)}, bf16[52,16,128]{2,1,0:T(8,128)(2,1)S(1)}, u32[]{:S(2)}, u32[]{:S(2)}) %collective-permute-start.14) | collective-permute-done | bytes 213024 | tf_op jit(solution)/shard_map/ppermute | solution.py:550
  79.4 2.1 %collective-permute-start.16 = (bf16[13,16,128]{2,1,0:T(8,128)(2,1)S(1)}, bf16[13,16,128]{2,1,0:T(8,128)(2,1)S(1)}, u32[]{:S(2)}, u32[]{:S(2)}) collective-permute-start(bf16[13,16,128]{2,1,0:T(8,128)(2,1)S(1)} %get-tuple-element.70), channel_id=1, source_target_pairs={{0,4},{2,6},{4,0},{6,2},{8,12},{10,14},{12,8},{14,10},{1,5},{3,7},... | collective-permute-start | bytes 159752 | tf_op jit(solution)/shard_map/ppermute | solution.py:550
  84.0 3.5 %collective-permute-done.17 = bf16[13,16,128]{2,1,0:T(8,128)(2,1)S(1)} collective-permute-done((bf16[13,16,128]{2,1,0:T(8,128)(2,1)S(1)}, bf16[13,16,128]{2,1,0:T(8,128)(2,1)S(1)}, u32[]{:S(2)}, u32[]{:S(2)}) %collective-permute-start.17) | collective-permute-done | bytes 53280 | tf_op jit(solution)/shard_map/ppermute | solution.py:550
  90.7 2.4 %collective-permute-start.21 = (bf16[13,16,128]{2,1,0:T(8,128)(2,1)S(1)}, bf16[13,16,128]{2,1,0:T(8,128)(2,1)S(1)}, u32[]{:S(2)}, u32[]{:S(2)}) collective-permute-start(bf16[13,16,128]{2,1,0:T(8,128)(2,1)S(1)} %fusion.5), channel_id=1, source_target_pairs={{0,12},{2,14},{4,8},{6,10},{8,4},{10,6},{12,0},{14,2},{1,13},{3,15... | collective-permute-start | bytes 159752 | tf_op jit(solution)/shard_map/ppermute | solution.py:550
  94.4 2.2 %collective-permute-done.21 = bf16[13,16,128]{2,1,0:T(8,128)(2,1)S(1)} collective-permute-done((bf16[13,16,128]{2,1,0:T(8,128)(2,1)S(1)}, bf16[13,16,128]{2,1,0:T(8,128)(2,1)S(1)}, u32[]{:S(2)}, u32[]{:S(2)}) %collective-permute-start.21) | collective-permute-done | bytes 53280 | tf_op jit(solution)/shard_map/ppermute | solution.py:550
  100.2 3.2 %collective-permute-done.22 = bf16[52,16,128]{2,1,0:T(8,128)(2,1)S(1)} collective-permute-done((bf16[52,16,128]{2,1,0:T(8,128)(2,1)S(1)}, bf16[52,16,128]{2,1,0:T(8,128)(2,1)S(1)}, u32[]{:S(2)}, u32[]{:S(2)}) %collective-permute-start.22) | collective-permute-done | bytes 213024 | tf_op jit(solution)/shard_map/ppermute | solution.py:550
  103.4 3.4 %collective-permute-done.23 = bf16[52,16,128]{2,1,0:T(8,128)(2,1)S(1)} collective-permute-done((bf16[52,16,128]{2,1,0:T(8,128)(2,1)S(1)}, bf16[52,16,128]{2,1,0:T(8,128)(2,1)S(1)}, u32[]{:S(2)}, u32[]{:S(2)}) %collective-permute-start.23) | collective-permute-done | bytes 213024 | tf_op jit(solution)/shard_map/ppermute | solution.py:550
  (62 shorter events, 28.5 us)
Async XLA Ops:
  0.6 35.2 %collective-permute-start.2 = (bf16[1,256,2048]{2,1,0:T(8,128)(2,1)}, bf16[1,256,2048]{2,1,0:T(8,128)(2,1)S(1)}, u32[]{:S(2)}, u32[]{:S(2)}) collective-permute-start(bf16[1,256,2048]{2,1,0:T(8,128)(2,1)} %param.14), channel_id=1, source_target_pairs={{0,16},{16,0},{1,17},{17,1},{2,18},{18,2},{3,19},{19,3},{4,20},{20... | collective-permute-start | bytes 3145736 | tf_op jit(solution)/shard_map/ppermute | solution.py:33
  5.1 12.7 %collective-permute-start.3 = (bf16[256,640]{1,0:T(8,128)(2,1)S(1)}, bf16[256,640]{1,0:T(8,128)(2,1)S(1)}, u32[]{:S(2)}, u32[]{:S(2)}) collective-permute-start(bf16[256,640]{1,0:T(8,128)(2,1)S(1)} %get-tuple-element.41.a_ref.refs_2_), channel_id=1, source_target_pairs={{0,4},{2,6},{4,8},{6,10},{8,12},{10,14},{1,5},{3,7},{5,9},{7,11},{... | collective-permute-start | bytes 983048 | tf_op jit(solution)/shard_map/ppermute | solution.py:28
  9.8 14.1 %collective-permute-start.7 = (bf16[256,512]{1,0:T(8,128)(2,1)S(1)}, bf16[256,512]{1,0:T(8,128)(2,1)S(1)}, u32[]{:S(2)}, u32[]{:S(2)}) collective-permute-start(bf16[256,512]{1,0:T(8,128)(2,1)S(1)} %get-tuple-element.44.a_ref.refs_2_), channel_id=1, source_target_pairs={{0,4},{2,6},{4,8},{6,10},{8,12},{10,14},{1,5},{3,7},{5,9},{7,11},{... | collective-permute-start | bytes 786440 | tf_op jit(solution)/shard_map/ppermute | solution.py:28
  13.2 15.8 %collective-permute-start.5 = (bf16[256,512]{1,0:T(8,128)(2,1)S(1)}, bf16[256,512]{1,0:T(8,128)(2,1)S(1)}, u32[]{:S(2)}, u32[]{:S(2)}) collective-permute-start(bf16[256,512]{1,0:T(8,128)(2,1)S(1)} %get-tuple-element.43.a_ref.refs_2_), channel_id=1, source_target_pairs={{0,4},{2,6},{4,8},{6,10},{8,12},{10,14},{1,5},{3,7},{5,9},{7,11},{... | collective-permute-start | bytes 786440 | tf_op jit(solution)/shard_map/ppermute | solution.py:28
  17.9 17.9 %collective-permute-start.4 = (bf16[256,640]{1,0:T(8,128)(2,1)S(1)}, bf16[256,640]{1,0:T(8,128)(2,1)S(1)}, u32[]{:S(2)}, u32[]{:S(2)}) collective-permute-start(bf16[256,640]{1,0:T(8,128)(2,1)S(1)} %choose.5), channel_id=1, source_target_pairs={{0,2},{2,0},{4,6},{6,4},{8,10},{10,8},{12,14},{14,12},{1,3},{3,1},... | collective-permute-start | bytes 983048 | tf_op jit(solution)/shard_map/ppermute | solution.py:38
  19.4 14.8 %collective-permute-start = (bf16[256,512]{1,0:T(8,128)(2,1)S(1)}, bf16[256,512]{1,0:T(8,128)(2,1)S(1)}, u32[]{:S(2)}, u32[]{:S(2)}) collective-permute-start(bf16[256,512]{1,0:T(8,128)(2,1)S(1)} %get-tuple-element.35.a_ref.refs_2_), channel_id=1, source_target_pairs={{0,4},{2,6},{4,8},{6,10},{8,12},{10,14},{1,5},{3,7},{5,9},{7,11},{... | collective-permute-start | bytes 786440 | tf_op jit(solution)/shard_map/ppermute | solution.py:28
  23.9 16.4 %collective-permute-start.8 = (bf16[256,512]{1,0:T(8,128)(2,1)S(1)}, bf16[256,512]{1,0:T(8,128)(2,1)S(1)}, u32[]{:S(2)}, u32[]{:S(2)}) collective-permute-start(bf16[256,512]{1,0:T(8,128)(2,1)S(1)} %choose.7), channel_id=1, source_target_pairs={{0,2},{2,0},{4,6},{6,4},{8,10},{10,8},{12,14},{14,12},{1,3},{3,1},... | collective-permute-start | bytes 786440 | tf_op jit(solution)/shard_map/ppermute | solution.py:38
  29.1 15.0 %collective-permute-start.6 = (bf16[256,512]{1,0:T(8,128)(2,1)S(1)}, bf16[256,512]{1,0:T(8,128)(2,1)S(1)}, u32[]{:S(2)}, u32[]{:S(2)}) collective-permute-start(bf16[256,512]{1,0:T(8,128)(2,1)S(1)} %choose.6), channel_id=1, source_target_pairs={{0,2},{2,0},{4,6},{6,4},{8,10},{10,8},{12,14},{14,12},{1,3},{3,1},... | collective-permute-start | bytes 786440 | tf_op jit(solution)/shard_map/ppermute | solution.py:38
  34.2 14.0 %collective-permute-start.1 = (bf16[256,512]{1,0:T(8,128)(2,1)S(1)}, bf16[256,512]{1,0:T(8,128)(2,1)S(1)}, u32[]{:S(2)}, u32[]{:S(2)}) collective-permute-start(bf16[256,512]{1,0:T(8,128)(2,1)S(1)} %choose.4), channel_id=1, source_target_pairs={{0,2},{2,0},{4,6},{6,4},{8,10},{10,8},{12,14},{14,12},{1,3},{3,1},... | collective-permute-start | bytes 786440 | tf_op jit(solution)/shard_map/ppermute | solution.py:38
  52.2 8.1 %collective-permute-start.11 = (bf16[256,2048]{1,0:T(8,128)(2,1)S(1)}, bf16[256,2048]{1,0:T(8,128)(2,1)S(1)}, u32[]{:S(2)}, u32[]{:S(2)}) collective-permute-start(bf16[256,2048]{1,0:T(8,128)(2,1)S(1)} %get-tuple-element.59), channel_id=1, source_target_pairs={{0,16},{16,0},{1,17},{17,1},{2,18},{18,2},{3,19},{19,3},{4,20},{20... | collective-permute-start | bytes 3145736 | tf_op jit(solution)/shard_map/ppermute | solution.py:33
  52.2 5.6 %collective-permute-start.10 = (bf16[32,256]{1,0:T(8,128)(2,1)S(1)}, bf16[32,256]{1,0:T(8,128)(2,1)S(1)}, u32[]{:S(2)}, u32[]{:S(2)}) collective-permute-start(bf16[32,256]{1,0:T(8,128)(2,1)S(1)} %get-tuple-element.56), channel_id=1, source_target_pairs={{2,0},{4,2},{6,4},{8,6},{10,8},{12,10},{14,12},{3,1},{5,3},{7,5},{... | collective-permute-start | bytes 49160 | tf_op jit(solution)/shard_map/ppermute | solution.py:28
  53.5 6.7 %collective-permute-start.9 = (bf16[32,256]{1,0:T(8,128)(2,1)S(1)}, bf16[32,256]{1,0:T(8,128)(2,1)S(1)}, u32[]{:S(2)}, u32[]{:S(2)}) collective-permute-start(bf16[32,256]{1,0:T(8,128)(2,1)S(1)} %get-tuple-element.55), channel_id=1, source_target_pairs={{4,0},{6,2},{8,4},{10,6},{12,8},{14,10},{5,1},{7,3},{9,5},{11,7},{... | collective-permute-start | bytes 49160 | tf_op jit(solution)/shard_map/ppermute | solution.py:28
  65.6 8.2 %collective-permute-start.13 = (bf16[52,16,128]{2,1,0:T(8,128)(2,1)S(1)}, bf16[52,16,128]{2,1,0:T(8,128)(2,1)S(1)}, u32[]{:S(2)}, u32[]{:S(2)}) collective-permute-start(bf16[52,16,128]{2,1,0:T(8,128)(2,1)S(1)} %get-tuple-element.67), channel_id=1, source_target_pairs={{0,2},{1,3},{2,0},{3,1},{4,6},{5,7},{6,4},{7,5},{8,10},{9,11},{10,... | collective-permute-start | bytes 638984 | tf_op jit(solution)/shard_map/ppermute | solution.py:550
  67.7 11.6 %collective-permute-start.14 = (bf16[52,16,128]{2,1,0:T(8,128)(2,1)S(1)}, bf16[52,16,128]{2,1,0:T(8,128)(2,1)S(1)}, u32[]{:S(2)}, u32[]{:S(2)}) collective-permute-start(bf16[52,16,128]{2,1,0:T(8,128)(2,1)S(1)} %get-tuple-element.69), channel_id=1, source_target_pairs={{0,1},{1,0},{2,3},{3,2},{4,5},{5,4},{6,7},{7,6},{8,9},{9,8},{10,11... | collective-permute-start | bytes 638984 | tf_op jit(solution)/shard_map/ppermute | solution.py:550
  69.2 10.1 %collective-permute-start.15 = (bf16[52,16,128]{2,1,0:T(8,128)(2,1)S(1)}, bf16[52,16,128]{2,1,0:T(8,128)(2,1)S(1)}, u32[]{:S(2)}, u32[]{:S(2)}) collective-permute-start(bf16[52,16,128]{2,1,0:T(8,128)(2,1)S(1)} %get-tuple-element.68), channel_id=1, source_target_pairs={{0,3},{1,2},{2,1},{3,0},{4,7},{5,6},{6,5},{7,4},{8,11},{9,10},{10,... | collective-permute-start | bytes 638984 | tf_op jit(solution)/shard_map/ppermute | solution.py:550
  79.4 4.6 %collective-permute-start.16 = (bf16[13,16,128]{2,1,0:T(8,128)(2,1)S(1)}, bf16[13,16,128]{2,1,0:T(8,128)(2,1)S(1)}, u32[]{:S(2)}, u32[]{:S(2)}) collective-permute-start(bf16[13,16,128]{2,1,0:T(8,128)(2,1)S(1)} %get-tuple-element.70), channel_id=1, source_target_pairs={{0,4},{2,6},{4,0},{6,2},{8,12},{10,14},{12,8},{14,10},{1,5},{3,7},... | collective-permute-start | bytes 159752 | tf_op jit(solution)/shard_map/ppermute | solution.py:550
  81.5 6.0 %collective-permute-start.17 = (bf16[13,16,128]{2,1,0:T(8,128)(2,1)S(1)}, bf16[13,16,128]{2,1,0:T(8,128)(2,1)S(1)}, u32[]{:S(2)}, u32[]{:S(2)}) collective-permute-start(bf16[13,16,128]{2,1,0:T(8,128)(2,1)S(1)} %get-tuple-element.72), channel_id=1, source_target_pairs={{0,8},{2,10},{4,12},{6,14},{8,0},{10,2},{12,4},{14,6},{1,9},{3,11}... | collective-permute-start | bytes 159752 | tf_op jit(solution)/shard_map/ppermute | solution.py:550
  82.6 6.0 %collective-permute-start.18 = (bf16[13,16,128]{2,1,0:T(8,128)(2,1)S(1)}, bf16[13,16,128]{2,1,0:T(8,128)(2,1)S(1)}, u32[]{:S(2)}, u32[]{:S(2)}) collective-permute-start(bf16[13,16,128]{2,1,0:T(8,128)(2,1)S(1)} %get-tuple-element.71), channel_id=1, source_target_pairs={{0,12},{2,14},{4,8},{6,10},{8,4},{10,6},{12,0},{14,2},{1,13},{3,15... | collective-permute-start | bytes 159752 | tf_op jit(solution)/shard_map/ppermute | solution.py:550
  88.6 4.8 %collective-permute-start.19 = (bf16[13,16,128]{2,1,0:T(8,128)(2,1)S(1)}, bf16[13,16,128]{2,1,0:T(8,128)(2,1)S(1)}, u32[]{:S(2)}, u32[]{:S(2)}) collective-permute-start(bf16[13,16,128]{2,1,0:T(8,128)(2,1)S(1)} %fusion.5), channel_id=1, source_target_pairs={{0,4},{2,6},{4,0},{6,2},{8,12},{10,14},{12,8},{14,10},{1,5},{3,7},... | collective-permute-start | bytes 159752 | tf_op jit(solution)/shard_map/ppermute | solution.py:550
  89.3 5.0 %collective-permute-start.20 = (bf16[13,16,128]{2,1,0:T(8,128)(2,1)S(1)}, bf16[13,16,128]{2,1,0:T(8,128)(2,1)S(1)}, u32[]{:S(2)}, u32[]{:S(2)}) collective-permute-start(bf16[13,16,128]{2,1,0:T(8,128)(2,1)S(1)} %fusion.5), channel_id=1, source_target_pairs={{0,8},{2,10},{4,12},{6,14},{8,0},{10,2},{12,4},{14,6},{1,9},{3,11}... | collective-permute-start | bytes 159752 | tf_op jit(solution)/shard_map/ppermute | solution.py:550
  90.7 5.9 %collective-permute-start.21 = (bf16[13,16,128]{2,1,0:T(8,128)(2,1)S(1)}, bf16[13,16,128]{2,1,0:T(8,128)(2,1)S(1)}, u32[]{:S(2)}, u32[]{:S(2)}) collective-permute-start(bf16[13,16,128]{2,1,0:T(8,128)(2,1)S(1)} %fusion.5), channel_id=1, source_target_pairs={{0,12},{2,14},{4,8},{6,10},{8,4},{10,6},{12,0},{14,2},{1,13},{3,15... | collective-permute-start | bytes 159752 | tf_op jit(solution)/shard_map/ppermute | solution.py:550
  96.6 6.8 %collective-permute-start.22 = (bf16[52,16,128]{2,1,0:T(8,128)(2,1)S(1)}, bf16[52,16,128]{2,1,0:T(8,128)(2,1)S(1)}, u32[]{:S(2)}, u32[]{:S(2)}) collective-permute-start(bf16[52,16,128]{2,1,0:T(8,128)(2,1)S(1)} %bitcast.74), channel_id=1, source_target_pairs={{0,2},{1,3},{2,0},{3,1},{4,6},{5,7},{6,4},{7,5},{8,10},{9,11},{10,... | collective-permute-start | bytes 638984 | tf_op jit(solution)/shard_map/ppermute | solution.py:550
  98.2 8.6 %collective-permute-start.23 = (bf16[52,16,128]{2,1,0:T(8,128)(2,1)S(1)}, bf16[52,16,128]{2,1,0:T(8,128)(2,1)S(1)}, u32[]{:S(2)}, u32[]{:S(2)}) collective-permute-start(bf16[52,16,128]{2,1,0:T(8,128)(2,1)S(1)} %bitcast.75), channel_id=1, source_target_pairs={{0,1},{1,0},{2,3},{3,2},{4,5},{5,4},{6,7},{7,6},{8,9},{9,8},{10,11... | collective-permute-start | bytes 638984 | tf_op jit(solution)/shard_map/ppermute | solution.py:550
  98.7 8.0 %collective-permute-start.24 = (bf16[52,16,128]{2,1,0:T(8,128)(2,1)S(1)}, bf16[52,16,128]{2,1,0:T(8,128)(2,1)S(1)}, u32[]{:S(2)}, u32[]{:S(2)}) collective-permute-start(bf16[52,16,128]{2,1,0:T(8,128)(2,1)S(1)} %bitcast.76), channel_id=1, source_target_pairs={{0,3},{1,2},{2,1},{3,0},{4,7},{5,6},{6,5},{7,4},{8,11},{9,10},{10,... | collective-permute-start | bytes 638984 | tf_op jit(solution)/shard_map/ppermute | solution.py:550
  (8 other events, 157.3 us)

commit v2 on v1

--- a/solution.py
+++ b/solution.py
@@ -75,34 +75,39 @@
     first = place_ref[1]
 
     def labels(position):
-        docs = jnp.zeros(position.shape, jnp.int32)
-        tenants = jnp.full(position.shape, adapter_ref[0, 0], jnp.int32)
+        label = jnp.full(position.shape, adapter_ref[0, 0], jnp.int32)
         end = jnp.int32(0)
-        for i in range(lengths_ref.shape[1]):
+        for i in range(lengths_ref.shape[1] - 1):
             end = end + lengths_ref[0, i]
-            past = end <= position
-            docs = docs + past.astype(jnp.int32)
-            if i + 1 < lengths_ref.shape[1]:
-                tenants = jnp.where(past, adapter_ref[0, i + 1], tenants)
-        return docs, tenants
+            label = jnp.where(end <= position, 64 * (i + 1) + adapter_ref[0, i + 1], label)
+        return label
 
     key_pos = first + lax.broadcasted_iota(jnp.int32, (span, HD), 0)
-    key_docs, key_tenants = labels(key_pos)
-    lane = lax.broadcasted_iota(jnp.int32, (span, HD), 1)
-    mask_ref[...] = ((lane // rank) % adapters == key_tenants).astype(f32).astype(bf16)
+    key_label = labels(key_pos)
+    lane = lax.broadcasted_iota(jnp.int32, (1, HD), 1)
+    mask_ref[...] = ((lane // rank) % adapters == (key_label & 63)).astype(f32).astype(bf16)
     pos = first + (span - tok) + lax.broadcasted_iota(jnp.int32, (SUB, tok), 1)
-    docs, tenants = labels(pos)
+    label = labels(pos)[:1]
     row = lax.broadcasted_iota(jnp.int32, (width, tok), 0)
-    own_mask_ref[...] = ((row // rank) % adapters == tenants[:1]).astype(f32)
+    own_mask_ref[...] = ((row // rank) % adapters == (label & 63)).astype(f32)
     for c in range(0, tok, HD):
         lanes = slice(c, c + HD)
         gap = pos[:1, lanes] - key_pos
-        allowed = (key_docs == docs[:1, lanes]) & (gap >= 0) & (gap < WINDOW) & (key_pos >= 0)
+        allowed = (key_label == label[:, lanes]) & (gap >= 0) & (gap < WINDOW) & (key_pos >= 0)
         bias_ref[:, lanes] = jnp.where(allowed, 0.0, masked_score)
-    angle = key_pos.astype(f32) * freq_ref[...]
-    cos_ref[...] = jnp.cos(angle)
-    sin = jnp.sin(angle)
-    sin_ref[...] = jnp.where(lane < HD // 2, -sin, sin)
+    size = next(n for n in (32, 16, 8, 1) if span % n == 0)
+    groups = span // size
+    padded = -(-groups // 8) * 8
+    freq = freq_ref[...]
+    outer = (first + size * lax.broadcasted_iota(jnp.int32, (padded, HD), 0)).astype(f32) * freq
+    inner = lax.broadcasted_iota(jnp.int32, (size, HD), 0).astype(f32) * freq
+    cos_o, sin_o, cos_i, sin_i = jnp.cos(outer), jnp.sin(outer), jnp.cos(inner), jnp.sin(inner)
+    sign = jnp.where(lane < HD // 2, -1.0, 1.0)
+    for k in range(groups):
+        rows = slice(k * size, (k + 1) * size)
+        c, s = cos_o[k : k + 1], sin_o[k : k + 1]
+        cos_ref[rows] = c * cos_i - s * sin_i
+        sin_ref[rows] = (sign * s) * cos_i + (sign * c) * sin_i
 
 
 def tables(place, lengths, adapter, span, tok, adapters, rank):

time: 112 us -> 112 us (level)
  waiting for transfers between devices: 38.4 us -> 40.2 us
  Pallas kernels: 28.8 us -> 27.1 us
    ppermute x6, waiting for transfers between devices: 10.8 us -> 12.6 us  [permute_by(): lax.ppermute(value, axis, [(i, i + steps) for i in range(first, last)])]
    pallas_call x1, Pallas kernels: 3.22 us -> 1.5 us  [tables(): pl.pallas_call(partial(tables_kernel, adapters=adapters, rank=rank), in_s...]
  transfers between devices with their start and end apart: 26 -> 26, of which waited for: 16 -> 16; matrix products, arithmetic and copies ran while one was open for 0% -> 0% of each run, Pallas kernels for 18% -> 17%
where the time goes in v2:
time: 112 us; the launch traced here: 111 us
  starting transfers between devices  41.4 us (37%)
  waiting for transfers between devices  40.2 us (36%)
  Pallas kernels  27.1 us (24%)
  local copies, waits for them, and re-layouts  1.14 us (1%)
    ppermute x12, waiting for transfers between devices, permute_masked(): return lax.ppermute(value, axes if len(axes) > 1 else axes[0], pairs)  24.8 us
    ppermute x6, starting transfers between devices, permute_by(): lax.ppermute(value, axis, [(i, i + steps) for i in range(first, last)])  18.6 us
    ppermute x12, starting transfers between devices, permute_masked(): return lax.ppermute(value, axes if len(axes) > 1 else axes[0], pairs)  16.2 us
    pallas_call x4, Pallas kernels, attention(): pl.pallas_call(partial(attention_kernel, n_blocks=n_blocks, first_head=fi...  15.3 us
    ppermute x6, waiting for transfers between devices, permute_by(): lax.ppermute(value, axis, [(i, i + steps) for i in range(first, last)])  12.6 us
    ppermute x4, starting transfers between devices, permute_xor(): return lax.ppermute(value, axis, [(i, i ^ bit) for i in range(count)])  5.83 us
    pallas_call x1, Pallas kernels, pack(): pl.pallas_call(partial(pack_kernel, pieces=pieces, lanes=lanes), in_specs...  3.8 us
    pallas_call x2, Pallas kernels, assemble(): pl.pallas_call(partial(assemble_kernel, cols=model_width // HD, rows=rows...  3.57 us
  transfers between devices with their start and end apart: 26, of which 16 were waited for; matrix products, arithmetic and copies ran while one was open for 0% of the time, Pallas kernels for 17%

profile of v2, /device:TPU:0, one launch (start us, length us, event | category | flops | bytes accessed | tf_op | source)
XLA Modules:
  0.0 111.3 jit_solution(3488916964107305534)
XLA Ops:
  1.3 3.8 %pack.1 = (bf16[256,640]{1,0:T(8,128)(2,1)S(1)}, bf16[256,512]{1,0:T(8,128)(2,1)S(1)}, bf16[256,512]{1,0:T(8,128)(2,1)S(1)}, bf16[256,512]{1,0:T(8,128)(2,1)S(1)}, s32[2]{0:T(128)S(4)}) custom-call(s32[2]{0:T(128)S(1)} %pad_add_fusion.place_ref, bf16[256,5376]{1,0:T(8,128)(2,1)} %bitcast.68, bf16[128,5376]{1,0:T(8,128)(2,1)} %bitcast.71, ...), custom_call_target="tpu_custom_call" | custom-call | tf_op jit(solution)/shard_map/pack/pallas_call | solution.py:192
  5.1 4.6 %collective-permute-start.3 = (bf16[256,640]{1,0:T(8,128)(2,1)S(1)}, bf16[256,640]{1,0:T(8,128)(2,1)S(1)}, u32[]{:S(2)}, u32[]{:S(2)}) collective-permute-start(bf16[256,640]{1,0:T(8,128)(2,1)S(1)} %get-tuple-element.41.a_ref.refs_2_), channel_id=1, source_target_pairs={{0,4},{2,6},{4,8},{6,10},{8,12},{10,14},{1,5},{3,7},{5,9},{7,11},{... | collective-permute-start | bytes 983048 | tf_op jit(solution)/shard_map/ppermute | solution.py:28
  9.8 3.5 %collective-permute-start.7 = (bf16[256,512]{1,0:T(8,128)(2,1)S(1)}, bf16[256,512]{1,0:T(8,128)(2,1)S(1)}, u32[]{:S(2)}, u32[]{:S(2)}) collective-permute-start(bf16[256,512]{1,0:T(8,128)(2,1)S(1)} %get-tuple-element.44.a_ref.refs_2_), channel_id=1, source_target_pairs={{0,4},{2,6},{4,8},{6,10},{8,12},{10,14},{1,5},{3,7},{5,9},{7,11},{... | collective-permute-start | bytes 786440 | tf_op jit(solution)/shard_map/ppermute | solution.py:28
  13.2 3.5 %collective-permute-start.5 = (bf16[256,512]{1,0:T(8,128)(2,1)S(1)}, bf16[256,512]{1,0:T(8,128)(2,1)S(1)}, u32[]{:S(2)}, u32[]{:S(2)}) collective-permute-start(bf16[256,512]{1,0:T(8,128)(2,1)S(1)} %get-tuple-element.43.a_ref.refs_2_), channel_id=1, source_target_pairs={{0,4},{2,6},{4,8},{6,10},{8,12},{10,14},{1,5},{3,7},{5,9},{7,11},{... | collective-permute-start | bytes 786440 | tf_op jit(solution)/shard_map/ppermute | solution.py:28
  19.4 4.4 %collective-permute-start = (bf16[256,512]{1,0:T(8,128)(2,1)S(1)}, bf16[256,512]{1,0:T(8,128)(2,1)S(1)}, u32[]{:S(2)}, u32[]{:S(2)}) collective-permute-start(bf16[256,512]{1,0:T(8,128)(2,1)S(1)} %get-tuple-element.35.a_ref.refs_2_), channel_id=1, source_target_pairs={{0,4},{2,6},{4,8},{6,10},{8,12},{10,14},{1,5},{3,7},{5,9},{7,11},{... | collective-permute-start | bytes 786440 | tf_op jit(solution)/shard_map/ppermute | solution.py:28
  25.0 4.0 %collective-permute-done.5.b_ref.refs_0_ = bf16[256,512]{1,0:T(8,128)(2,1)S(1)} collective-permute-done((bf16[256,512]{1,0:T(8,128)(2,1)S(1)}, bf16[256,512]{1,0:T(8,128)(2,1)S(1)}, u32[]{:S(2)}, u32[]{:S(2)}) %collective-permute-start.5) | collective-permute-done | bytes 262176 | tf_op jit(solution)/shard_map/ppermute | solution.py:28
  32.2 2.0 %collective-permute-done.b_ref.refs_0_ = bf16[256,512]{1,0:T(8,128)(2,1)S(1)} collective-permute-done((bf16[256,512]{1,0:T(8,128)(2,1)S(1)}, bf16[256,512]{1,0:T(8,128)(2,1)S(1)}, u32[]{:S(2)}, u32[]{:S(2)}) %collective-permute-start) | collective-permute-done | bytes 262176 | tf_op jit(solution)/shard_map/ppermute | solution.py:28
  36.8 3.5 %attention.4 = (bf16[256,2048]{1,0:T(8,128)(2,1)S(1)}, bf16[2,64,1024]{2,1,0:T(8,128)(2,1)S(1)}, f32[768,128]{1,0:T(8,128)S(1)}, bf16[768,128]{1,0:T(8,128)(2,1)S(1)}) custom-call(bf16[256,640]{1,0:T(8,128)(2,1)S(1)} %collective-permute-done.3.b_ref.refs_0_, bf16[256,640]{1,0:T(8,128)(2,1)S(1)} %collective-permute-done.4.refs_1_, ...), custom_call_target="tpu_custom_call" | custom-call | flops 1006632960 | bytes 1310720 | tf_op jit(solution)/shard_map/attention/pallas_call | solution.py:396
  40.2 3.9 %attention.5 = (bf16[256,2048]{1,0:T(8,128)(2,1)S(1)}, bf16[2,64,1024]{2,1,0:T(8,128)(2,1)S(1)}, f32[768,128]{1,0:T(8,128)S(1)}) custom-call(bf16[256,512]{1,0:T(8,128)(2,1)S(1)} %collective-permute-done.7.b_ref.refs_0_, bf16[256,512]{1,0:T(8,128)(2,1)S(1)} %collective-permute-done.8.refs_1_, ...), custom_call_target="tpu_custom_call", output_to_operand_aliasing={{0}: (12, {}), {1}: (13, {}), {2}: (11, {})} | custom-call | flops 1006632960 | bytes 1310720 | tf_op jit(solution)/shard_map/attention/pallas_call | solution.py:396
  44.1 3.9 %attention.6 = (bf16[256,2048]{1,0:T(8,128)(2,1)S(1)}, bf16[2,64,1024]{2,1,0:T(8,128)(2,1)S(1)}, f32[768,128]{1,0:T(8,128)S(1)}) custom-call(bf16[256,512]{1,0:T(8,128)(2,1)S(1)} %collective-permute-done.5.b_ref.refs_0_, bf16[256,512]{1,0:T(8,128)(2,1)S(1)} %collective-permute-done.6.refs_1_, ...), custom_call_target="tpu_custom_call", output_to_operand_aliasing={{0}: (12, {}), {1}: (13, {}), {2}: (11, {})} | custom-call | flops 1006632960 | bytes 1310720 | tf_op jit(solution)/shard_map/attention/pallas_call | solution.py:396
  48.0 4.1 %attention.7 = (bf16[256,2048]{1,0:T(8,128)(2,1)S(1)}, bf16[2,64,1024]{2,1,0:T(8,128)(2,1)S(1)}, bf16[32,256]{1,0:T(8,128)(2,1)S(1)}, bf16[32,256]{1,0:T(8,128)(2,1)S(1)}, bf16[32,256]{1,0:T(8,128)(2,1)S(1)}) custom-call(bf16[256,512]{1,0:T(8,128)(2,1)S(1)} %collective-permute-done.b_ref.refs_0_, ...), custom_call_target="tpu_custom_call", output_to_operand_aliasing={{0}: (12, {}), {1}: (13, {})} | custom-call | flops 1006632960 | bytes 1310720 | tf_op jit(solution)/shard_map/attention/pallas_call | solution.py:396
  54.8 3.0 %collective-permute-done.10.refs_3_ = bf16[32,256]{1,0:T(8,128)(2,1)S(1)} collective-permute-done((bf16[32,256]{1,0:T(8,128)(2,1)S(1)}, bf16[32,256]{1,0:T(8,128)(2,1)S(1)}, u32[]{:S(2)}, u32[]{:S(2)}) %collective-permute-start.10) | collective-permute-done | bytes 16416 | tf_op jit(solution)/shard_map/ppermute | solution.py:28
  57.8 2.4 %collective-permute-done.9.refs_2_ = bf16[32,256]{1,0:T(8,128)(2,1)S(1)} collective-permute-done((bf16[32,256]{1,0:T(8,128)(2,1)S(1)}, bf16[32,256]{1,0:T(8,128)(2,1)S(1)}, u32[]{:S(2)}, u32[]{:S(2)}) %collective-permute-start.9) | collective-permute-done | bytes 16416 | tf_op jit(solution)/shard_map/ppermute | solution.py:28
  60.2 2.6 %product.1 = (bf16[208,16,128]{2,1,0:T(8,128)(2,1)S(1)}, bf16[208,16,128]{2,1,0:T(8,128)(2,1)S(1)}, bf16[1,256,2048]{2,1,0:T(8,128)(2,1)}) custom-call(s32[1]{0:T(128)} %bitcast.refs_0_, bf16[32,256]{1,0:T(8,128)(2,1)S(1)} %get-tuple-element.54.refs_1_, bf16[32,256]{1,0:T(8,128)(2,1)S(1)} %collective-permute-done.9.refs_2_, ...), custom_call_target="tpu_custom_call" | custom-call | tf_op jit(solution)/shard_map/product/pallas_call | solution.py:650
  62.9 2.3 %collective-permute-done.12.recv_ref = bf16[208,16,128]{2,1,0:T(8,128)(2,1)S(1)} collective-permute-done((bf16[208,16,128]{2,1,0:T(8,128)(2,1)S(1)}, bf16[208,16,128]{2,1,0:T(8,128)(2,1)S(1)}, u32[]{:S(2)}, u32[]{:S(2)}) %collective-permute-start.12) | collective-permute-done | bytes 852000 | tf_op jit(solution)/shard_map/ppermute | solution.py:33
  65.6 2.1 %collective-permute-start.13 = (bf16[52,16,128]{2,1,0:T(8,128)(2,1)S(1)}, bf16[52,16,128]{2,1,0:T(8,128)(2,1)S(1)}, u32[]{:S(2)}, u32[]{:S(2)}) collective-permute-start(bf16[52,16,128]{2,1,0:T(8,128)(2,1)S(1)} %get-tuple-element.67), channel_id=1, source_target_pairs={{0,2},{1,3},{2,0},{3,1},{4,6},{5,7},{6,4},{7,5},{8,10},{9,11},{10,... | collective-permute-start | bytes 638984 | tf_op jit(solution)/shard_map/ppermute | solution.py:555
  69.2 4.6 %collective-permute-done.13 = bf16[52,16,128]{2,1,0:T(8,128)(2,1)S(1)} collective-permute-done((bf16[52,16,128]{2,1,0:T(8,128)(2,1)S(1)}, bf16[52,16,128]{2,1,0:T(8,128)(2,1)S(1)}, u32[]{:S(2)}, u32[]{:S(2)}) %collective-permute-start.13) | collective-permute-done | bytes 213024 | tf_op jit(solution)/shard_map/ppermute | solution.py:555
  73.8 5.5 %collective-permute-done.14 = bf16[52,16,128]{2,1,0:T(8,128)(2,1)S(1)} collective-permute-done((bf16[52,16,128]{2,1,0:T(8,128)(2,1)S(1)}, bf16[52,16,128]{2,1,0:T(8,128)(2,1)S(1)}, u32[]{:S(2)}, u32[]{:S(2)}) %collective-permute-start.14) | collective-permute-done | bytes 213024 | tf_op jit(solution)/shard_map/ppermute | solution.py:555
  79.4 2.1 %collective-permute-start.16 = (bf16[13,16,128]{2,1,0:T(8,128)(2,1)S(1)}, bf16[13,16,128]{2,1,0:T(8,128)(2,1)S(1)}, u32[]{:S(2)}, u32[]{:S(2)}) collective-permute-start(bf16[13,16,128]{2,1,0:T(8,128)(2,1)S(1)} %get-tuple-element.70), channel_id=1, source_target_pairs={{0,4},{2,6},{4,0},{6,2},{8,12},{10,14},{12,8},{14,10},{1,5},{3,7},... | collective-permute-start | bytes 159752 | tf_op jit(solution)/shard_map/ppermute | solution.py:555
  83.9 3.5 %collective-permute-done.17 = bf16[13,16,128]{2,1,0:T(8,128)(2,1)S(1)} collective-permute-done((bf16[13,16,128]{2,1,0:T(8,128)(2,1)S(1)}, bf16[13,16,128]{2,1,0:T(8,128)(2,1)S(1)}, u32[]{:S(2)}, u32[]{:S(2)}) %collective-permute-start.17) | collective-permute-done | bytes 53280 | tf_op jit(solution)/shard_map/ppermute | solution.py:555
  90.6 2.4 %collective-permute-start.21 = (bf16[13,16,128]{2,1,0:T(8,128)(2,1)S(1)}, bf16[13,16,128]{2,1,0:T(8,128)(2,1)S(1)}, u32[]{:S(2)}, u32[]{:S(2)}) collective-permute-start(bf16[13,16,128]{2,1,0:T(8,128)(2,1)S(1)} %fusion.5), channel_id=1, source_target_pairs={{0,12},{2,14},{4,8},{6,10},{8,4},{10,6},{12,0},{14,2},{1,13},{3,15... | collective-permute-start | bytes 159752 | tf_op jit(solution)/shard_map/ppermute | solution.py:555
  94.3 2.2 %collective-permute-done.21 = bf16[13,16,128]{2,1,0:T(8,128)(2,1)S(1)} collective-permute-done((bf16[13,16,128]{2,1,0:T(8,128)(2,1)S(1)}, bf16[13,16,128]{2,1,0:T(8,128)(2,1)S(1)}, u32[]{:S(2)}, u32[]{:S(2)}) %collective-permute-start.21) | collective-permute-done | bytes 53280 | tf_op jit(solution)/shard_map/ppermute | solution.py:555
  100.2 3.2 %collective-permute-done.22 = bf16[52,16,128]{2,1,0:T(8,128)(2,1)S(1)} collective-permute-done((bf16[52,16,128]{2,1,0:T(8,128)(2,1)S(1)}, bf16[52,16,128]{2,1,0:T(8,128)(2,1)S(1)}, u32[]{:S(2)}, u32[]{:S(2)}) %collective-permute-start.22) | collective-permute-done | bytes 213024 | tf_op jit(solution)/shard_map/ppermute | solution.py:555
  103.4 3.4 %collective-permute-done.23 = bf16[52,16,128]{2,1,0:T(8,128)(2,1)S(1)} collective-permute-done((bf16[52,16,128]{2,1,0:T(8,128)(2,1)S(1)}, bf16[52,16,128]{2,1,0:T(8,128)(2,1)S(1)}, u32[]{:S(2)}, u32[]{:S(2)}) %collective-permute-start.23) | collective-permute-done | bytes 213024 | tf_op jit(solution)/shard_map/ppermute | solution.py:555
  (62 shorter events, 29.7 us)
Async XLA Ops:
  0.6 35.2 %collective-permute-start.2 = (bf16[1,256,2048]{2,1,0:T(8,128)(2,1)}, bf16[1,256,2048]{2,1,0:T(8,128)(2,1)S(1)}, u32[]{:S(2)}, u32[]{:S(2)}) collective-permute-start(bf16[1,256,2048]{2,1,0:T(8,128)(2,1)} %param.14), channel_id=1, source_target_pairs={{0,16},{16,0},{1,17},{17,1},{2,18},{18,2},{3,19},{19,3},{4,20},{20... | collective-permute-start | bytes 3145736 | tf_op jit(solution)/shard_map/ppermute | solution.py:33
  5.1 12.7 %collective-permute-start.3 = (bf16[256,640]{1,0:T(8,128)(2,1)S(1)}, bf16[256,640]{1,0:T(8,128)(2,1)S(1)}, u32[]{:S(2)}, u32[]{:S(2)}) collective-permute-start(bf16[256,640]{1,0:T(8,128)(2,1)S(1)} %get-tuple-element.41.a_ref.refs_2_), channel_id=1, source_target_pairs={{0,4},{2,6},{4,8},{6,10},{8,12},{10,14},{1,5},{3,7},{5,9},{7,11},{... | collective-permute-start | bytes 983048 | tf_op jit(solution)/shard_map/ppermute | solution.py:28
  9.8 14.1 %collective-permute-start.7 = (bf16[256,512]{1,0:T(8,128)(2,1)S(1)}, bf16[256,512]{1,0:T(8,128)(2,1)S(1)}, u32[]{:S(2)}, u32[]{:S(2)}) collective-permute-start(bf16[256,512]{1,0:T(8,128)(2,1)S(1)} %get-tuple-element.44.a_ref.refs_2_), channel_id=1, source_target_pairs={{0,4},{2,6},{4,8},{6,10},{8,12},{10,14},{1,5},{3,7},{5,9},{7,11},{... | collective-permute-start | bytes 786440 | tf_op jit(solution)/shard_map/ppermute | solution.py:28
  13.2 15.8 %collective-permute-start.5 = (bf16[256,512]{1,0:T(8,128)(2,1)S(1)}, bf16[256,512]{1,0:T(8,128)(2,1)S(1)}, u32[]{:S(2)}, u32[]{:S(2)}) collective-permute-start(bf16[256,512]{1,0:T(8,128)(2,1)S(1)} %get-tuple-element.43.a_ref.refs_2_), channel_id=1, source_target_pairs={{0,4},{2,6},{4,8},{6,10},{8,12},{10,14},{1,5},{3,7},{5,9},{7,11},{... | collective-permute-start | bytes 786440 | tf_op jit(solution)/shard_map/ppermute | solution.py:28
  17.9 17.9 %collective-permute-start.4 = (bf16[256,640]{1,0:T(8,128)(2,1)S(1)}, bf16[256,640]{1,0:T(8,128)(2,1)S(1)}, u32[]{:S(2)}, u32[]{:S(2)}) collective-permute-start(bf16[256,640]{1,0:T(8,128)(2,1)S(1)} %choose.5), channel_id=1, source_target_pairs={{0,2},{2,0},{4,6},{6,4},{8,10},{10,8},{12,14},{14,12},{1,3},{3,1},... | collective-permute-start | bytes 983048 | tf_op jit(solution)/shard_map/ppermute | solution.py:38
  19.4 14.8 %collective-permute-start = (bf16[256,512]{1,0:T(8,128)(2,1)S(1)}, bf16[256,512]{1,0:T(8,128)(2,1)S(1)}, u32[]{:S(2)}, u32[]{:S(2)}) collective-permute-start(bf16[256,512]{1,0:T(8,128)(2,1)S(1)} %get-tuple-element.35.a_ref.refs_2_), channel_id=1, source_target_pairs={{0,4},{2,6},{4,8},{6,10},{8,12},{10,14},{1,5},{3,7},{5,9},{7,11},{... | collective-permute-start | bytes 786440 | tf_op jit(solution)/shard_map/ppermute | solution.py:28
  23.9 16.4 %collective-permute-start.8 = (bf16[256,512]{1,0:T(8,128)(2,1)S(1)}, bf16[256,512]{1,0:T(8,128)(2,1)S(1)}, u32[]{:S(2)}, u32[]{:S(2)}) collective-permute-start(bf16[256,512]{1,0:T(8,128)(2,1)S(1)} %choose.7), channel_id=1, source_target_pairs={{0,2},{2,0},{4,6},{6,4},{8,10},{10,8},{12,14},{14,12},{1,3},{3,1},... | collective-permute-start | bytes 786440 | tf_op jit(solution)/shard_map/ppermute | solution.py:38
  29.1 15.0 %collective-permute-start.6 = (bf16[256,512]{1,0:T(8,128)(2,1)S(1)}, bf16[256,512]{1,0:T(8,128)(2,1)S(1)}, u32[]{:S(2)}, u32[]{:S(2)}) collective-permute-start(bf16[256,512]{1,0:T(8,128)(2,1)S(1)} %choose.6), channel_id=1, source_target_pairs={{0,2},{2,0},{4,6},{6,4},{8,10},{10,8},{12,14},{14,12},{1,3},{3,1},... | collective-permute-start | bytes 786440 | tf_op jit(solution)/shard_map/ppermute | solution.py:38
  34.2 13.8 %collective-permute-start.1 = (bf16[256,512]{1,0:T(8,128)(2,1)S(1)}, bf16[256,512]{1,0:T(8,128)(2,1)S(1)}, u32[]{:S(2)}, u32[]{:S(2)}) collective-permute-start(bf16[256,512]{1,0:T(8,128)(2,1)S(1)} %choose.4), channel_id=1, source_target_pairs={{0,2},{2,0},{4,6},{6,4},{8,10},{10,8},{12,14},{14,12},{1,3},{3,1},... | collective-permute-start | bytes 786440 | tf_op jit(solution)/shard_map/ppermute | solution.py:38
  52.1 8.1 %collective-permute-start.11 = (bf16[256,2048]{1,0:T(8,128)(2,1)S(1)}, bf16[256,2048]{1,0:T(8,128)(2,1)S(1)}, u32[]{:S(2)}, u32[]{:S(2)}) collective-permute-start(bf16[256,2048]{1,0:T(8,128)(2,1)S(1)} %get-tuple-element.59), channel_id=1, source_target_pairs={{0,16},{16,0},{1,17},{17,1},{2,18},{18,2},{3,19},{19,3},{4,20},{20... | collective-permute-start | bytes 3145736 | tf_op jit(solution)/shard_map/ppermute | solution.py:33
  52.2 5.6 %collective-permute-start.10 = (bf16[32,256]{1,0:T(8,128)(2,1)S(1)}, bf16[32,256]{1,0:T(8,128)(2,1)S(1)}, u32[]{:S(2)}, u32[]{:S(2)}) collective-permute-start(bf16[32,256]{1,0:T(8,128)(2,1)S(1)} %get-tuple-element.56), channel_id=1, source_target_pairs={{2,0},{4,2},{6,4},{8,6},{10,8},{12,10},{14,12},{3,1},{5,3},{7,5},{... | collective-permute-start | bytes 49160 | tf_op jit(solution)/shard_map/ppermute | solution.py:28
  53.5 6.7 %collective-permute-start.9 = (bf16[32,256]{1,0:T(8,128)(2,1)S(1)}, bf16[32,256]{1,0:T(8,128)(2,1)S(1)}, u32[]{:S(2)}, u32[]{:S(2)}) collective-permute-start(bf16[32,256]{1,0:T(8,128)(2,1)S(1)} %get-tuple-element.55), channel_id=1, source_target_pairs={{4,0},{6,2},{8,4},{10,6},{12,8},{14,10},{5,1},{7,3},{9,5},{11,7},{... | collective-permute-start | bytes 49160 | tf_op jit(solution)/shard_map/ppermute | solution.py:28
  65.6 8.2 %collective-permute-start.13 = (bf16[52,16,128]{2,1,0:T(8,128)(2,1)S(1)}, bf16[52,16,128]{2,1,0:T(8,128)(2,1)S(1)}, u32[]{:S(2)}, u32[]{:S(2)}) collective-permute-start(bf16[52,16,128]{2,1,0:T(8,128)(2,1)S(1)} %get-tuple-element.67), channel_id=1, source_target_pairs={{0,2},{1,3},{2,0},{3,1},{4,6},{5,7},{6,4},{7,5},{8,10},{9,11},{10,... | collective-permute-start | bytes 638984 | tf_op jit(solution)/shard_map/ppermute | solution.py:555
  67.6 11.6 %collective-permute-start.14 = (bf16[52,16,128]{2,1,0:T(8,128)(2,1)S(1)}, bf16[52,16,128]{2,1,0:T(8,128)(2,1)S(1)}, u32[]{:S(2)}, u32[]{:S(2)}) collective-permute-start(bf16[52,16,128]{2,1,0:T(8,128)(2,1)S(1)} %get-tuple-element.69), channel_id=1, source_target_pairs={{0,1},{1,0},{2,3},{3,2},{4,5},{5,4},{6,7},{7,6},{8,9},{9,8},{10,11... | collective-permute-start | bytes 638984 | tf_op jit(solution)/shard_map/ppermute | solution.py:555
  69.2 10.1 %collective-permute-start.15 = (bf16[52,16,128]{2,1,0:T(8,128)(2,1)S(1)}, bf16[52,16,128]{2,1,0:T(8,128)(2,1)S(1)}, u32[]{:S(2)}, u32[]{:S(2)}) collective-permute-start(bf16[52,16,128]{2,1,0:T(8,128)(2,1)S(1)} %get-tuple-element.68), channel_id=1, source_target_pairs={{0,3},{1,2},{2,1},{3,0},{4,7},{5,6},{6,5},{7,4},{8,11},{9,10},{10,... | collective-permute-start | bytes 638984 | tf_op jit(solution)/shard_map/ppermute | solution.py:555
  79.4 4.6 %collective-permute-start.16 = (bf16[13,16,128]{2,1,0:T(8,128)(2,1)S(1)}, bf16[13,16,128]{2,1,0:T(8,128)(2,1)S(1)}, u32[]{:S(2)}, u32[]{:S(2)}) collective-permute-start(bf16[13,16,128]{2,1,0:T(8,128)(2,1)S(1)} %get-tuple-element.70), channel_id=1, source_target_pairs={{0,4},{2,6},{4,0},{6,2},{8,12},{10,14},{12,8},{14,10},{1,5},{3,7},... | collective-permute-start | bytes 159752 | tf_op jit(solution)/shard_map/ppermute | solution.py:555
  81.5 6.0 %collective-permute-start.17 = (bf16[13,16,128]{2,1,0:T(8,128)(2,1)S(1)}, bf16[13,16,128]{2,1,0:T(8,128)(2,1)S(1)}, u32[]{:S(2)}, u32[]{:S(2)}) collective-permute-start(bf16[13,16,128]{2,1,0:T(8,128)(2,1)S(1)} %get-tuple-element.72), channel_id=1, source_target_pairs={{0,8},{2,10},{4,12},{6,14},{8,0},{10,2},{12,4},{14,6},{1,9},{3,11}... | collective-permute-start | bytes 159752 | tf_op jit(solution)/shard_map/ppermute | solution.py:555
  82.6 6.0 %collective-permute-start.18 = (bf16[13,16,128]{2,1,0:T(8,128)(2,1)S(1)}, bf16[13,16,128]{2,1,0:T(8,128)(2,1)S(1)}, u32[]{:S(2)}, u32[]{:S(2)}) collective-permute-start(bf16[13,16,128]{2,1,0:T(8,128)(2,1)S(1)} %get-tuple-element.71), channel_id=1, source_target_pairs={{0,12},{2,14},{4,8},{6,10},{8,4},{10,6},{12,0},{14,2},{1,13},{3,15... | collective-permute-start | bytes 159752 | tf_op jit(solution)/shard_map/ppermute | solution.py:555
  88.6 4.8 %collective-permute-start.19 = (bf16[13,16,128]{2,1,0:T(8,128)(2,1)S(1)}, bf16[13,16,128]{2,1,0:T(8,128)(2,1)S(1)}, u32[]{:S(2)}, u32[]{:S(2)}) collective-permute-start(bf16[13,16,128]{2,1,0:T(8,128)(2,1)S(1)} %fusion.5), channel_id=1, source_target_pairs={{0,4},{2,6},{4,0},{6,2},{8,12},{10,14},{12,8},{14,10},{1,5},{3,7},... | collective-permute-start | bytes 159752 | tf_op jit(solution)/shard_map/ppermute | solution.py:555
  89.3 5.0 %collective-permute-start.20 = (bf16[13,16,128]{2,1,0:T(8,128)(2,1)S(1)}, bf16[13,16,128]{2,1,0:T(8,128)(2,1)S(1)}, u32[]{:S(2)}, u32[]{:S(2)}) collective-permute-start(bf16[13,16,128]{2,1,0:T(8,128)(2,1)S(1)} %fusion.5), channel_id=1, source_target_pairs={{0,8},{2,10},{4,12},{6,14},{8,0},{10,2},{12,4},{14,6},{1,9},{3,11}... | collective-permute-start | bytes 159752 | tf_op jit(solution)/shard_map/ppermute | solution.py:555
  90.6 5.9 %collective-permute-start.21 = (bf16[13,16,128]{2,1,0:T(8,128)(2,1)S(1)}, bf16[13,16,128]{2,1,0:T(8,128)(2,1)S(1)}, u32[]{:S(2)}, u32[]{:S(2)}) collective-permute-start(bf16[13,16,128]{2,1,0:T(8,128)(2,1)S(1)} %fusion.5), channel_id=1, source_target_pairs={{0,12},{2,14},{4,8},{6,10},{8,4},{10,6},{12,0},{14,2},{1,13},{3,15... | collective-permute-start | bytes 159752 | tf_op jit(solution)/shard_map/ppermute | solution.py:555
  96.6 6.8 %collective-permute-start.22 = (bf16[52,16,128]{2,1,0:T(8,128)(2,1)S(1)}, bf16[52,16,128]{2,1,0:T(8,128)(2,1)S(1)}, u32[]{:S(2)}, u32[]{:S(2)}) collective-permute-start(bf16[52,16,128]{2,1,0:T(8,128)(2,1)S(1)} %bitcast.74), channel_id=1, source_target_pairs={{0,2},{1,3},{2,0},{3,1},{4,6},{5,7},{6,4},{7,5},{8,10},{9,11},{10,... | collective-permute-start | bytes 638984 | tf_op jit(solution)/shard_map/ppermute | solution.py:555
  98.2 8.6 %collective-permute-start.23 = (bf16[52,16,128]{2,1,0:T(8,128)(2,1)S(1)}, bf16[52,16,128]{2,1,0:T(8,128)(2,1)S(1)}, u32[]{:S(2)}, u32[]{:S(2)}) collective-permute-start(bf16[52,16,128]{2,1,0:T(8,128)(2,1)S(1)} %bitcast.75), channel_id=1, source_target_pairs={{0,1},{1,0},{2,3},{3,2},{4,5},{5,4},{6,7},{7,6},{8,9},{9,8},{10,11... | collective-permute-start | bytes 638984 | tf_op jit(solution)/shard_map/ppermute | solution.py:555
  98.7 8.0 %collective-permute-start.24 = (bf16[52,16,128]{2,1,0:T(8,128)(2,1)S(1)}, bf16[52,16,128]{2,1,0:T(8,128)(2,1)S(1)}, u32[]{:S(2)}, u32[]{:S(2)}) collective-permute-start(bf16[52,16,128]{2,1,0:T(8,128)(2,1)S(1)} %bitcast.76), channel_id=1, source_target_pairs={{0,3},{1,2},{2,1},{3,0},{4,7},{5,6},{6,5},{7,4},{8,11},{9,10},{10,... | collective-permute-start | bytes 638984 | tf_op jit(solution)/shard_map/ppermute | solution.py:555
  (8 other events, 157.3 us)
